TPU v7x, 256 devices: a whole 4x4x8 slice. The times are simulated.
256 devices in a mesh: row: 16 (over x, y_hi, core), col: 16 (over y_lo, z).
Axes of the slice: x: 4, y: 4 (y_hi: 2, y_lo: 2; y = y_hi * 2 + y_lo), z: 8, core: 2. Of those that a mesh axis runs over, the one named last changes fastest.
Arguments:
- field: float32 [1, 256, 256, 512], P(None, 'row', 'col'), may hold values from -6 to 6
- shell: int32 [256, 256, 256], P(('row', 'col')), may hold values from 0 to 255
Outputs:
- power_modes: float32 [1, 256, 256, 256], P(None, ('row', 'col'))
- spectrum: float32 [1, 256], replicated
All inputs are finite; a program needn't handle non-finite values.
Results may differ from a plain program's by a relative error of at most 0.0003.
Values sent between devices are 32-bit elements; how exact they have to be, the bound alone decides.
No kernel may reach another device: no remote copies, remote signals or barrier semaphores. Data moves between devices by JAX's collectives and lax.ppermute only.
A program may use at most 64 MiB of HBM per device.

v0:
```python
import functools
import math

import jax
import jax.numpy as jnp
from jax import lax
from jax.sharding import Mesh
from jax.sharding import PartitionSpec as P

SHELLS = 256
ROW = ("row_0", "row_1", "row_2")
COL = ("col_0", "col_1")
ROW_COL = ("row_0", "row_1", "row_2", "col_0", "col_1")


HIGH = lax.Precision.HIGHEST


def by_axis(shard, axes):
    return functools.reduce(lax.psum, axes, shard)


def tables(length, freqs):
    places = lax.iota(jnp.int32, length)
    phase = places[:, None] * freqs[None, :] % length
    angle = phase.astype(jnp.float32) * (2.0 * math.pi / length)
    factor = 1.0 / math.sqrt(length)
    return (jnp.cos(angle) * factor, -jnp.sin(angle) * factor)


def split_three(values):
    upper = values.astype(jnp.bfloat16)
    upper_back = lax.optimization_barrier(upper).astype(jnp.float32)
    rest = values - upper_back
    middle = rest.astype(jnp.bfloat16)
    middle_back = lax.optimization_barrier(middle).astype(jnp.float32)
    lowest = (rest - middle_back).astype(jnp.bfloat16)
    return jnp.concatenate([upper, middle, lowest], axis=0)


def local(field, shell):
    fields, cx, cy, nz = field.shape
    n_row = lax.axis_size(ROW)
    n_col = lax.axis_size(COL)
    nx = cx * n_row
    ny = cy * n_col
    keep = nz // 2
    planes = keep // (n_row * n_col)
    cos_x, sin_x = tables(nx, lax.iota(jnp.int32, nx))
    cos_y, sin_y = tables(ny, lax.iota(jnp.int32, ny))
    cos_z, sin_z = tables(nz, lax.iota(jnp.int32, keep))
    real = jnp.einsum("fxyz,zk->fyxk", field, cos_z, precision=HIGH)
    imag = jnp.einsum("fxyz,zk->fyxk", field, sin_z, precision=HIGH)
    cos_four = cos_x.reshape(n_row, cx, nx)
    sin_four = sin_x.reshape(n_row, cx, nx)
    a_re = lax.all_to_all(real, ROW, split_axis=3, concat_axis=3, tiled=True)
    a_im = lax.all_to_all(imag, ROW, split_axis=3, concat_axis=3, tiled=True)
    count = a_re.shape[1]
    a_re = a_re.reshape(fields, count, cx, n_row, keep // n_row)
    a_im = a_im.reshape(fields, count, cx, n_row, keep // n_row)
    o_re = jnp.einsum("fiasq,sak->fiqk", a_re, cos_four, precision=HIGH) - jnp.einsum(
        "fiasq,sak->fiqk", a_im, sin_four, precision=HIGH
    )
    o_im = jnp.einsum("fiasq,sak->fiqk", a_re, sin_four, precision=HIGH) + jnp.einsum(
        "fiasq,sak->fiqk", a_im, cos_four, precision=HIGH
    )
    real = o_re
    imag = o_im
    b_re = lax.all_to_all(real, COL, split_axis=2, concat_axis=1, tiled=True)
    b_im = lax.all_to_all(imag, COL, split_axis=2, concat_axis=1, tiled=True)
    o_re = jnp.einsum("fypi,yq->fpqi", b_re, cos_y, precision=HIGH) - jnp.einsum(
        "fypi,yq->fpqi", b_im, sin_y, precision=HIGH
    )
    o_im = jnp.einsum("fypi,yq->fpqi", b_re, sin_y, precision=HIGH) + jnp.einsum(
        "fypi,yq->fpqi", b_im, cos_y, precision=HIGH
    )
    power = o_re * o_re + o_im * o_im
    total = planes * ny * nx
    width = math.gcd(total, 32768)
    flat = power.reshape(fields, total)
    labels = shell.reshape(total)
    shell_ids = lax.iota(jnp.int32, SHELLS)

    def add_block(index, summed):
        start = index * width
        part = lax.dynamic_slice_in_dim(flat, start, width, 1)
        marks = lax.dynamic_slice_in_dim(labels, start, width, 0)
        onehot = (marks[:, None] == shell_ids[None, :]).astype(jnp.bfloat16)
        pieces = split_three(part)
        return summed + jnp.dot(pieces, onehot, preferred_element_type=jnp.float32)

    stacked = lax.fori_loop(
        0, total // width, add_block, jnp.zeros((3 * fields, SHELLS), jnp.float32)
    )
    sums = jnp.sum(stacked.reshape(3, fields, SHELLS), axis=0)
    sums = by_axis(sums, ROW_COL)
    spectrum = sums * (float(SHELLS) / (keep * ny * nx))
    return (power, spectrum)


def solution(mesh):
    split = Mesh(mesh.devices.reshape(4, 2, 2, 2, 8), ("row_0", "row_1", "row_2", "col_0", "col_1"))
    in_specs = (P(None, ROW, COL, None), P(ROW_COL, None, None))
    out_specs = (P(None, ROW_COL, None, None), P())
    return jax.shard_map(local, mesh=split, in_specs=in_specs, out_specs=out_specs, check_vma=False)
```

profile of v0, /device:TPU:8, one launch (start us, length us, event | category | flops | bytes accessed | tf_op | source)
XLA Modules:
  0.0 158.3 jit_solution(5042138185276069008)
XLA Ops:
  0.6 0.0 copy-start
  0.6 1.0 copy-done
  1.7 2.6 %convolution_bitcast_fusion.3 = f32[1,16,16,256]{3,1,2,0:T(8,128)S(1)} fusion(f32[1,16,16,512]{3,2,1,0:T(8,128)S(1)} %copy-done), kind=kOutput, calls=%fused_computation.24 | convolution fusion | flops 404750336 | bytes 786432 | tf_op jit(solution)/shard_map/fxyz,zk->fyxk/dot_general | solution.py:53
  4.3 1.3 copy.21
  5.5 1.5 reshape.101
  7.0 6.1 %all-to-all-start.1 = ((f32[16,1,4096]{2,1,0:T(1,128)}), f32[16,1,4096]{2,1,0:T(1,128)S(1)}, u32[]{:S(2)}, u32[]{:S(2)}) async-start(f32[16,1,4096]{2,1,0:T(1,128)} %reshape.101), calls=%async_computation.1 | async-start | bytes 524288 | tf_op jit(solution)/shard_map/all_to_all | solution.py:57
  13.1 2.6 %convolution_bitcast_fusion.5 = f32[1,16,16,256]{3,1,2,0:T(8,128)S(1)} fusion(f32[1,16,16,512]{3,2,1,0:T(8,128)S(1)} %copy-done), kind=kOutput, calls=%fused_computation.26 | convolution fusion | flops 404619264 | bytes 786432 | tf_op jit(solution)/shard_map/fxyz,zk->fyxk/dot_general | solution.py:52
  15.7 1.3 copy.18
  17.0 1.5 reshape.103
  18.5 3.8 %all-to-all-done.1 = f32[16,1,4096]{2,1,0:T(1,128)S(1)} async-done(((f32[16,1,4096]{2,1,0:T(1,128)}), f32[16,1,4096]{2,1,0:T(1,128)S(1)}, u32[]{:S(2)}, u32[]{:S(2)}) %all-to-all-start.1) | async-done | bytes 262176 | tf_op jit(solution)/shard_map/all_to_all | solution.py:57
  22.3 3.7 %all-to-all-start = ((f32[16,1,4096]{2,1,0:T(1,128)}), f32[16,1,4096]{2,1,0:T(1,128)S(1)}, u32[]{:S(2)}, u32[]{:S(2)}) async-start(f32[16,1,4096]{2,1,0:T(1,128)} %reshape.103), calls=%async_computation | async-start | bytes 524288 | tf_op jit(solution)/shard_map/all_to_all | solution.py:56
  26.0 0.5 broadcast.172
  26.6 1.3 reduce.2
  27.8 0.7 reshape.102
  28.5 2.9 %copy.30 = f32[16,16,16,16]{3,2,1,0:T(8,128)} copy(f32[16,16,16,16]{0,1,3,2:T(8,128)S(1)} %bitcast.88) | data formatting | bytes 524288 | tf_op jit(solution)/shard_map/reshape.6
  31.4 3.6 %all-to-all-done = f32[16,1,4096]{2,1,0:T(1,128)S(1)} async-done(((f32[16,1,4096]{2,1,0:T(1,128)}), f32[16,1,4096]{2,1,0:T(1,128)S(1)}, u32[]{:S(2)}, u32[]{:S(2)}) %all-to-all-start) | async-done | bytes 262176 | tf_op jit(solution)/shard_map/all_to_all | solution.py:56
  35.0 1.3 reduce.3
  36.3 2.0 %reshape.104 = f32[256,1,16,16]{3,2,1,0:T(8,128)} reshape(f32[16,4096]{1,0:T(8,128)S(1)} %reduce.3) | data formatting | bytes 524288
  38.3 3.0 %copy.28 = f32[16,16,16,16]{3,2,1,0:T(8,128)S(1)} copy(f32[16,16,16,16]{0,1,3,2:T(8,128)} %bitcast.89) | data formatting | bytes 524288 | tf_op jit(solution)/shard_map/reshape.2
  41.3 5.9 %convolution_bitcast_fusion.2 = f32[16,16,256]{2,1,0:T(8,128)S(1)} fusion(f32[16,16,16,16]{3,2,1,0:T(8,128)} %copy.30, s32[16,16]{0,1:T(8,128)S(1)} %multiply_add_fusion), kind=kOutput, calls=%fused_computation.23 | convolution fusion | flops 202375168 | bytes 525312 | tf_op jit(solution)/shard_map/fiasq,sak->fiqk/dot_general | solution.py:61
  47.2 4.3 %fusion.17 = f32[1,16,16,256]{3,2,1,0:T(8,128)S(1)} fusion(f32[16,16,256]{2,1,0:T(8,128)S(1)} %convolution_bitcast_fusion.2, f32[16,16,16,16]{3,2,1,0:T(8,128)S(1)} %copy.28, s32[16,16]{0,1:T(8,128)S(1)} %multiply_add_fusion), kind=kOutput, calls=%fused_computation.28 | convolution fusion | flops 202375168 | bytes 787456 | tf_op jit(solution)/shard_map/fiasq,sak->fiqk/dot_general | solution.py:61
  51.5 0.9 copy.24
  52.4 9.9 %all-to-all-start.2 = ((f32[1,16,16,256]{3,1,0,2:T(8,128)}), f32[1,16,16,256]{3,1,0,2:T(8,128)S(1)}, u32[]{:S(2)}, u32[]{:S(2)}) async-start(f32[1,16,16,256]{3,1,0,2:T(8,128)} %copy.24), calls=%async_computation.2 | async-start | bytes 524288 | tf_op jit(solution)/shard_map/all_to_all | solution.py:69
  62.3 5.9 %convolution_bitcast_fusion = f32[16,16,256]{2,1,0:T(8,128)S(1)} fusion(f32[16,16,16,16]{3,2,1,0:T(8,128)} %copy.30, s32[16,16]{0,1:T(8,128)S(1)} %multiply_add_fusion), kind=kOutput, calls=%fused_computation.21 | convolution fusion | flops 202309632 | bytes 525312 | tf_op jit(solution)/shard_map/fiasq,sak->fiqk/dot_general | solution.py:64
  68.2 0.0 copy-start.1
  68.2 4.3 %fusion.19 = f32[1,16,16,256]{3,2,1,0:T(8,128)S(1)} fusion(f32[16,16,256]{2,1,0:T(8,128)S(1)} %convolution_bitcast_fusion, f32[16,16,16,16]{3,2,1,0:T(8,128)S(1)} %copy.28, s32[16,16]{0,1:T(8,128)S(1)} %multiply_add_fusion), kind=kOutput, calls=%fused_computation.30 | convolution fusion | flops 202440704 | bytes 787456 | tf_op jit(solution)/shard_map/fiasq,sak->fiqk/dot_general | solution.py:64
  72.5 0.8 copy.27
  73.3 0.0 all-to-all-done.2
  73.4 8.1 %all-to-all-start.3 = ((f32[1,16,16,256]{3,1,0,2:T(8,128)}), f32[1,16,16,256]{3,1,0,2:T(8,128)S(1)}, u32[]{:S(2)}, u32[]{:S(2)}) async-start(f32[1,16,16,256]{3,1,0,2:T(8,128)} %copy.27), calls=%async_computation.3 | async-start | bytes 524288 | tf_op jit(solution)/shard_map/all_to_all | solution.py:70
  81.5 0.0 copy-done.1
  81.5 0.1 copy.47
  81.6 1.8 %fusion.55 = f32[256,256]{1,0:T(8,128)S(1)} fusion(f32[256,256]{1,0:T(8,128)S(1)} %bitcast.92), kind=kOutput, calls=%fused_computation.77 | convolution fusion | flops 202309632 | bytes 524288 | tf_op jit(solution)/shard_map/fypi,yq->fpqi/dot_general | solution.py:71
  83.4 1.8 %fusion.56 = f32[256,256]{1,0:T(8,128)S(1)} fusion(f32[256,256]{1,0:T(8,128)S(1)} %bitcast.93), kind=kOutput, calls=%fused_computation.78 | convolution fusion | flops 202375168 | bytes 524288 | tf_op jit(solution)/shard_map/fypi,yq->fpqi/dot_general | solution.py:74
  85.2 5.4 %all-to-all-done.3 = f32[1,16,16,256]{3,1,0,2:T(8,128)S(1)} async-done(((f32[1,16,16,256]{3,1,0,2:T(8,128)}), f32[1,16,16,256]{3,1,0,2:T(8,128)S(1)}, u32[]{:S(2)}, u32[]{:S(2)}) %all-to-all-start.3) | async-done | bytes 262176 | tf_op jit(solution)/shard_map/all_to_all | solution.py:70
  90.7 1.8 %fusion.15 = f32[256,256]{1,0:T(8,128)S(1)} fusion(f32[256,256]{1,0:T(8,128)S(1)} %fusion.55, f32[256,256]{1,0:T(8,128)S(1)} %bitcast.94), kind=kOutput, calls=%fused_computation.20 | convolution fusion | flops 202506240 | bytes 786432 | tf_op jit(solution)/shard_map/fypi,yq->fpqi/dot_general | solution.py:71
  92.5 1.8 %fusion.14 = f32[1,1,256,256]{3,2,1,0:T(8,128)S(1)} fusion(f32[256,256]{1,0:T(8,128)S(1)} %fusion.15, f32[256,256]{1,0:T(8,128)S(1)} %fusion.56, f32[256,256]{1,0:T(8,128)S(1)} %bitcast.95), kind=kOutput, calls=%fused_computation.18 | convolution fusion | flops 202506240 | bytes 1048576 | tf_op jit(solution)/shard_map/fypi,yq->fpqi/dot_general | solution.py:74
  94.3 0.0 copy-start.2
  94.3 0.3 copy.46
  94.6 0.4 copy-done.2
  95.0 23.8 %while.14 = (s32[]{:T(128)}, f32[3,256]{1,0:T(4,128)S(1)}, f32[1,65536]{1,0:T(1,128)S(1)}, s32[65536]{0:T(1024)S(1)}, s32[]{:T(128)}, /*index=5*/s32[]{:T(128)}, s32[]{:T(128)}, s32[]{:T(128)}) while((s32[]{:T(128)}, f32[3,256]{1,0:T(4,128)S(1)}, f32[1,65536]{1,0:T(1,128)S(1)}, s32[65536]{0:T(1024)S(1)}, s32[]{:T(128)}, ...), condition=%wide.region_1.2_spmd.clone, body=%wide.region_0.1_spmd.clone.sunk | while | flops 59573768 | bytes 1317021 | solution.py:92
  95.0 0.1 dynamic-slice_convert_fusion.2
  95.1 0.2 fusion.135
  95.3 0.2 subtract_convert_fusion.2
  95.5 11.4 %fusion.136 = f32[3,256]{1,0:T(4,128)S(1)} fusion(s32[32768]{0:T(1024)S(1)} %dynamic_slice.29, bf16[1,32768]{1,0:T(2,128)(2,1)S(1)} %subtract_convert_fusion.2, bf16[1,32768]{1,0:T(2,128)(2,1)S(1)} %fusion.135, bf16[1,32768]{1,0:T(2,128)(2,1)S(1)} %dynamic-slice_convert_fusion.2, f32[3,256]{1,0:T(4,128)S(1)} %get-tuple-element.156, pred[]{:T(512)S(6)} %compare.6), kind=kOutput, calls=%fused_computation.4.clone.1 | convolution fusion | flops 59311616 | bytes 333825 | tf_op jit(solution)/shard_map/while/body/eval_jaxpr/dot_general | solution.py:90
  106.9 0.1 dynamic-slice_convert_fusion.2
  107.0 0.2 fusion.135
  107.2 0.2 subtract_convert_fusion.2
  107.5 11.4 %fusion.136 = f32[3,256]{1,0:T(4,128)S(1)} fusion(s32[32768]{0:T(1024)S(1)} %dynamic_slice.29, bf16[1,32768]{1,0:T(2,128)(2,1)S(1)} %subtract_convert_fusion.2, bf16[1,32768]{1,0:T(2,128)(2,1)S(1)} %fusion.135, bf16[1,32768]{1,0:T(2,128)(2,1)S(1)} %dynamic-slice_convert_fusion.2, f32[3,256]{1,0:T(4,128)S(1)} %get-tuple-element.156, pred[]{:T(512)S(6)} %compare.6), kind=kOutput, calls=%fused_computation.4.clone.1 | convolution fusion | flops 59311616 | bytes 333825 | tf_op jit(solution)/shard_map/while/body/eval_jaxpr/dot_general | solution.py:90
  118.8 8.8 %psum.35 = f32[1,256]{1,0:T(1,128)S(1)} all-reduce(f32[1,256]{1,0:T(1,128)S(1)} %bitcast.96), channel_id=1, replica_groups=mesh['row_0'=4,'row_1'=2,'row_2'=2,'col_0'=2,'col_1'=8] {'row_0'}, use_global_device_ids=true, to_apply=%region_3.4 | all-reduce | flops 256 | bytes 2048 | tf_op jit(solution)/shard_map/psum | solution.py:20
  127.7 6.4 %psum.36 = f32[1,256]{1,0:T(1,128)S(1)} all-reduce(f32[1,256]{1,0:T(1,128)S(1)} %psum.35), channel_id=1, replica_groups=mesh['row_0'=4,'row_1'=2,'row_2'=2,'col_0'=2,'col_1'=8] {'row_1'}, use_global_device_ids=true, to_apply=%region_4.5 | all-reduce | flops 256 | bytes 2048 | tf_op jit(solution)/shard_map/psum | solution.py:20
  134.1 2.4 %psum.37 = f32[1,256]{1,0:T(1,128)S(1)} all-reduce(f32[1,256]{1,0:T(1,128)S(1)} %psum.36), channel_id=1, replica_groups=mesh['row_0'=4,'row_1'=2,'row_2'=2,'col_0'=2,'col_1'=8] {'row_2'}, use_global_device_ids=true, to_apply=%region_5.6 | all-reduce | flops 256 | bytes 2048 | tf_op jit(solution)/shard_map/psum | solution.py:20
  136.5 4.9 %psum.38 = f32[1,256]{1,0:T(1,128)S(1)} all-reduce(f32[1,256]{1,0:T(1,128)S(1)} %psum.37), channel_id=1, replica_groups=mesh['row_0'=4,'row_1'=2,'row_2'=2,'col_0'=2,'col_1'=8] {'col_0'}, use_global_device_ids=true, to_apply=%region_6.7 | all-reduce | flops 256 | bytes 2048 | tf_op jit(solution)/shard_map/psum | solution.py:20
  141.4 16.3 %psum.39 = f32[1,256]{1,0:T(1,128)S(1)} all-reduce(f32[1,256]{1,0:T(1,128)S(1)} %psum.38), channel_id=1, replica_groups=mesh['row_0'=4,'row_1'=2,'row_2'=2,'col_0'=2,'col_1'=8] {'col_1'}, use_global_device_ids=true, to_apply=%region_7.8 | all-reduce | flops 256 | bytes 2048 | tf_op jit(solution)/shard_map/psum | solution.py:20
  157.7 0.6 broadcast_multiply_fusion
  (5 shorter events, 0.1 us)
Async XLA Ops:
  0.6 1.0 copy-start
  7.0 15.3 %all-to-all-start.1 = ((f32[16,1,4096]{2,1,0:T(1,128)}), f32[16,1,4096]{2,1,0:T(1,128)S(1)}, u32[]{:S(2)}, u32[]{:S(2)}) async-start(f32[16,1,4096]{2,1,0:T(1,128)} %reshape.101), calls=%async_computation.1 | async-start | bytes 524288 | tf_op jit(solution)/shard_map/all_to_all | solution.py:57
  22.3 12.7 %all-to-all-start = ((f32[16,1,4096]{2,1,0:T(1,128)}), f32[16,1,4096]{2,1,0:T(1,128)S(1)}, u32[]{:S(2)}, u32[]{:S(2)}) async-start(f32[16,1,4096]{2,1,0:T(1,128)} %reshape.103), calls=%async_computation | async-start | bytes 524288 | tf_op jit(solution)/shard_map/all_to_all | solution.py:56
  52.4 21.0 %all-to-all-start.2 = ((f32[1,16,16,256]{3,1,0,2:T(8,128)}), f32[1,16,16,256]{3,1,0,2:T(8,128)S(1)}, u32[]{:S(2)}, u32[]{:S(2)}) async-start(f32[1,16,16,256]{3,1,0,2:T(8,128)} %copy.24), calls=%async_computation.2 | async-start | bytes 524288 | tf_op jit(solution)/shard_map/all_to_all | solution.py:69
  68.2 13.3 %copy-start.1 = (s32[1,256,256]{2,1,0:T(8,128)S(1)}, s32[1,256,256]{2,1,0:T(8,128)}, u32[]{:S(2)}) copy-start(s32[1,256,256]{2,1,0:T(8,128)} %param.5) | copy-start | bytes 786436
  73.4 17.3 %all-to-all-start.3 = ((f32[1,16,16,256]{3,1,0,2:T(8,128)}), f32[1,16,16,256]{3,1,0,2:T(8,128)S(1)}, u32[]{:S(2)}, u32[]{:S(2)}) async-start(f32[1,16,16,256]{3,1,0,2:T(8,128)} %copy.27), calls=%async_computation.3 | async-start | bytes 524288 | tf_op jit(solution)/shard_map/all_to_all | solution.py:70
  94.3 0.7 copy-start.2
where the time goes:
time: 159 us; the launch traced here: 158 us
  matrix products  55.4 us (35%)
  blocking collectives  38.9 us (24%)
  starting transfers between devices  27.9 us (18%)
  local copies, waits for them, and re-layouts  18.4 us (12%)
  waiting for transfers between devices  12.9 us (8%)
  other arithmetic  3.96 us (2%)
    psum x5, blocking collectives, by_axis(): return functools.reduce(lax.psum, axes, shard)  38.9 us
    dot_general x2, matrix products, add_block(): return summed + jnp.dot(pieces, onehot, preferred_element_type=jnp.float32)  22.7 us
    all_to_all x1, starting transfers between devices, local(): b_re = lax.all_to_all(real, COL, split_axis=2, concat_axis=1, tiled=True)  9.94 us
    all_to_all x1, starting transfers between devices, local(): b_im = lax.all_to_all(imag, COL, split_axis=2, concat_axis=1, tiled=True)  8.13 us
    unnamed x12, local copies, waits for them, and re-layouts  7.53 us
    all_to_all x1, starting transfers between devices, local(): a_im = lax.all_to_all(imag, ROW, split_axis=3, concat_axis=3, tiled=True)  6.14 us
    dot_general x1, matrix products, local(): jnp.einsum('fiasq,sak->fiqk', a_im, sin_four, precision=HIGH)  5.89 us
    another operation x2, local copies, waits for them, and re-layouts  5.88 us
  transfers between devices with their start and end apart: 4, of which 3 were waited for; matrix products, arithmetic and copies ran while one was open for 16% of the time, Pallas kernels for 0%

commit v1 on v0

v1 whole, which is shorter than its diff:
```python
import functools
import math

import jax
import jax.numpy as jnp
import numpy as np
from jax import lax
from jax.experimental import pallas as pl
from jax.experimental.pallas import tpu as pltpu
from jax.sharding import Mesh
from jax.sharding import PartitionSpec as P

SHELLS = 256
ROW = ("row_0", "row_1", "row_2")
COL = ("col_0", "col_1")
ROW_COL = ROW + COL
F32 = jnp.float32
BF16 = jnp.bfloat16


def split_table(table):
    upper = table.astype(np.float32).astype(BF16)
    lower = (table - upper.astype(np.float64)).astype(np.float32).astype(BF16)
    return np.stack([upper, lower])


@functools.cache
def depth_tables(nz):
    half = nz // 2
    freqs = nz // 4
    z = np.arange(half)
    out = []
    for parity in range(2):
        k = 2 * np.arange(freqs) + parity
        angle = 2.0 * math.pi / nz * (k[:, None] * z[None, :] % nz)
        out.append(split_table(np.concatenate([np.cos(angle), -np.sin(angle)])))
    return np.stack(out)


@functools.cache
def plane_tables(radix):
    n = np.arange(radix)
    base = np.multiply.outer(n, n)
    both = base[:, None, :, None] + base[None, :, None, :]
    both = both.reshape(radix * radix, radix * radix)
    angle = 2.0 * math.pi / radix * (both % radix)
    square = np.stack([split_table(np.cos(angle)), split_table(-np.sin(angle))])
    angle = 2.0 * math.pi / (radix * radix) * (both % (radix * radix))
    twiddle = np.stack([np.cos(angle), -np.sin(angle)]).astype(np.float32)
    return square, twiddle


def split_two(values):
    upper = values.astype(BF16)
    return upper, (values - upper.astype(F32)).astype(BF16)


NN = (((1,), (0,)), ((), ()))
NT = (((1,), (1,)), ((), ()))


def dot3(lhs, rhs, dims):
    dot = functools.partial(lax.dot_general, dimension_numbers=dims, preferred_element_type=F32)
    return dot(lhs[0], rhs[0]) + dot(lhs[0], rhs[1]) + dot(lhs[1], rhs[0])


def depth_kernel(field_ref, table_ref, out_ref):
    half = field_ref.shape[1] // 2
    lanes = field_ref.shape[0] // 2
    freqs = table_ref.shape[2] // 2
    near = field_ref[:, :half]
    far = field_ref[:, half:]
    for parity in range(2):
        folded = split_two(near + far if parity == 0 else near - far)
        spec = dot3((table_ref[parity, 0], table_ref[parity, 1]), folded, NT)
        for part in range(2):
            for side in range(2):
                block = spec[part * freqs : (part + 1) * freqs, side * lanes : (side + 1) * lanes]
                out_ref[pl.ds(parity * 4 + part * 2 + side, freqs, stride=8), :] = block


def swap_digits(blocks, radix):
    lane = lax.broadcasted_iota(jnp.int32, blocks[0].shape, 1)
    width = blocks[0].shape[1]
    step = 1
    while step < radix:
        low = (lane & step) == 0
        out = list(blocks)
        for i in range(radix):
            if i & step:
                continue
            a, b = blocks[i], blocks[i + step]
            out[i] = jnp.where(low, a, pltpu.roll(b, step, 1))
            out[i + step] = jnp.where(low, pltpu.roll(a, width - step, 1), b)
        blocks = out
        step *= 2
    return blocks


def plane_kernel(scale, unit, recv_ref, square_ref, twiddle_ref, shell_ref, power_ref, sums_ref, acc_ref):
    n = power_ref.shape[0]
    radix = math.isqrt(n)
    parts = [
        jnp.concatenate([recv_ref[pl.ds(2 * c + s, n, stride=4), :] for s in range(2)], axis=1)
        for c in range(2)
    ]
    re, im = split_two(parts[0]), split_two(parts[1])
    cos = (square_ref[0, 0], square_ref[0, 1])
    sin = (square_ref[1, 0], square_ref[1, 1])
    u_re = dot3(cos, re, NN) - dot3(sin, im, NN)
    u_im = dot3(sin, re, NN) + dot3(cos, im, NN)
    t_re, t_im = twiddle_ref[0], twiddle_ref[1]
    re = split_two(u_re * t_re - u_im * t_im)
    im = split_two(u_re * t_im + u_im * t_re)
    v_re = dot3(re, cos, NN) - dot3(im, sin, NN)
    v_im = dot3(re, sin, NN) + dot3(im, cos, NN)
    power = (v_re * v_re + v_im * v_im) * scale
    half = n // 2
    for side in range(2):
        blocks = [
            power[a * radix : (a + 1) * radix, side * half : (side + 1) * half] for a in range(radix)
        ]
        for b, block in enumerate(swap_digits(blocks, radix)):
            power_ref[b * radix : (b + 1) * radix, side * half : (side + 1) * half] = block

    acc_ref[...] = jnp.zeros_like(acc_ref)

    def add_rows(index, carry):
        rows = pl.ds(index * 16, 16)
        upper, lower = split_two(power_ref[rows, :])
        marks = shell_ref[rows, :]
        high = (marks >> 4).astype(F32).astype(BF16)
        low = (marks & 15).astype(F32).astype(BF16)
        zero = jnp.zeros_like(upper)
        one = jnp.ones_like(upper)
        picks = [jnp.where(high == jnp.array(h, BF16), upper, zero) for h in range(16)]
        picks += [jnp.where(high == jnp.array(h, BF16), lower, zero) for h in range(16)]
        marked = [jnp.where(low == jnp.array(l, BF16), one, zero) for l in range(16)]
        acc_ref[...] += lax.dot_general(
            jnp.concatenate(picks, axis=0),
            jnp.concatenate(marked, axis=0),
            NT,
            preferred_element_type=F32,
        )
        return carry

    lax.fori_loop(0, n // 16, add_rows, 0)
    acc = acc_ref[:SHELLS, :] + acc_ref[SHELLS:, :]
    row = lax.broadcasted_iota(jnp.int32, (256, 256), 0)
    lane = lax.broadcasted_iota(jnp.int32, (256, 256), 1)
    same = jnp.where((row & 15) == (lane & 15), acc, 0.0)
    by_high = jnp.sum(same.reshape(16, 16, 256), axis=1)
    spread = ((row >> 4) == (lane & 15)).astype(F32).astype(BF16)
    upper = by_high.astype(BF16)
    rest = by_high - upper.astype(F32)
    middle, lower = split_two(rest)
    wide = sum(
        lax.dot_general(piece, spread, NN, preferred_element_type=F32)
        for piece in (upper, middle, lower)
    )
    row = lax.broadcasted_iota(jnp.int32, (16, 256), 0)
    lane = lax.broadcasted_iota(jnp.int32, (16, 256), 1)
    sums = jnp.sum(jnp.where((lane >> 4) == row, wide, 0.0), axis=0, keepdims=True) * unit
    for side in range(2):
        piece = sums[:, side * 128 : (side + 1) * 128]
        count = sums_ref.shape[0] // 2
        sums_ref[pl.ds(side, count, stride=2), :] = jnp.broadcast_to(piece, (count, 128))


def depth_call(field, tables):
    rows = field.shape[0]
    return pl.pallas_call(
        depth_kernel,
        out_shape=jax.ShapeDtypeStruct((field.shape[1] // 2 * 4, rows // 2), F32),
        name="depth",
    )(field, tables)


def plane_call(recv, square, twiddle, shell, devices, scale, unit):
    n = shell.shape[0]
    return pl.pallas_call(
        functools.partial(plane_kernel, scale, unit),
        out_shape=(
            jax.ShapeDtypeStruct((n, n), F32),
            jax.ShapeDtypeStruct((devices * 2, 128), F32),
        ),
        scratch_shapes=[pltpu.VMEM((2 * SHELLS, 256), F32)],
        name="plane",
    )(recv, square, twiddle, shell)


def local(field, shell):
    fields, cx, cy, nz = field.shape
    n_row = lax.axis_size(ROW)
    n_col = lax.axis_size(COL)
    devices = n_row * n_col
    nx, ny, keep = cx * n_row, cy * n_col, nz // 2
    square, twiddle = plane_tables(n_row)
    scale = 1.0 / (float(nx) * ny * nz)
    unit = float(SHELLS) / (keep * ny * nx)
    sent = depth_call(field.reshape(cx * cy, nz), depth_tables(nz))
    sent = sent.reshape(devices, 4, 128)
    got = lax.all_to_all(sent, ROW_COL, 0, 0, tiled=True)
    power, sums = plane_call(
        got.reshape(devices * 4, 128), square, twiddle, shell.reshape(ny, nx), devices, scale, unit
    )
    sums = lax.all_to_all(sums.reshape(devices, 2, 128), ROW_COL, 0, 0, tiled=True)
    spectrum = jnp.sum(sums, axis=0).reshape(fields, SHELLS)
    return (power.reshape(fields, 1, ny, nx), spectrum)


def solution(mesh):
    split = Mesh(mesh.devices.reshape(4, 2, 2, 2, 8), ROW_COL)
    in_specs = (P(None, ROW, COL, None), P(ROW_COL, None, None))
    out_specs = (P(None, ROW_COL, None, None), P())
    return jax.shard_map(local, mesh=split, in_specs=in_specs, out_specs=out_specs, check_vma=False)
```

time: 159 us -> 71 us (0.45)
  the two profiles are of different devices: /device:TPU:8 before, /device:TPU:1 now
where the time goes in v1:
time: 71 us; the launch traced here: 70.8 us
  blocking collectives  58.9 us (83%)
  Pallas kernels  10.4 us (15%)
  other arithmetic  0.84 us (1%)
    all_to_all x1, blocking collectives, local(): got = lax.all_to_all(sent, ROW_COL, 0, 0, tiled=True)  36.9 us
    all_to_all x1, blocking collectives, local(): lax.all_to_all(sums.reshape(devices, 2, 128), ROW_COL, 0, 0, tiled=True)  21.9 us
    pallas_call x1, Pallas kernels, plane_call(): pl.pallas_call(functools.partial(plane_kernel, scale, unit), out_shape=(j...  8 us
    pallas_call x1, Pallas kernels, depth_call(): pl.pallas_call(depth_kernel, out_shape=jax.ShapeDtypeStruct((field.shape[...  2.45 us

profile of v1, /device:TPU:1, one launch (start us, length us, event | category | flops | bytes accessed | tf_op | source)
XLA Modules:
  0.0 70.8 jit_solution(18214657184498213537)
XLA Ops:
  0.6 2.4 %depth.1 = f32[1024,128]{1,0:T(8,128)} custom-call(f32[256,512]{1,0:T(8,128)} %bitcast.9, bf16[2,2,256,256]{3,2,1,0:T(8,128)(2,1)} %constant.8.clone.table_ref), custom_call_target="tpu_custom_call" | custom-call | tf_op jit(solution)/shard_map/depth/pallas_call | solution.py:172
  3.1 36.9 %all_to_all.10 = f32[256,4,128]{2,1,0:T(4,128)} all-to-all(f32[256,4,128]{2,1,0:T(4,128)} %bitcast.8), channel_id=1, replica_groups=mesh['row_0'=4,'row_1'=2,'row_2'=2,'col_0'=2,'col_1'=8] {'row_0','row_1'..., dimensions={0} | all-to-all | bytes 1048576 | tf_op jit(solution)/shard_map/all_to_all | solution.py:203
  40.0 8.0 %plane.1 = (f32[256,256]{1,0:T(8,128)}, f32[512,128]{1,0:T(8,128)}) custom-call(f32[1024,128]{1,0:T(8,128)} %bitcast.7, bf16[2,2,256,256]{3,2,1,0:T(8,128)(2,1)} %constant.9.clone.square_ref, f32[2,256,256]{2,1,0:T(8,128)} %constant.10.clone.twiddle_ref, s32[256,256]{1,0:T(8,128)} %bitcast.10), custom_call_target="tpu_custom_call" | custom-call | tf_op jit(solution)/shard_map/plane/pallas_call | solution.py:181
  48.0 21.9 %all_to_all.11 = f32[256,2,128]{2,1,0:T(2,128)S(1)} all-to-all(f32[256,2,128]{2,1,0:T(2,128)} %bitcast.11), channel_id=1, replica_groups=mesh['row_0'=4,'row_1'=2,'row_2'=2,'col_0'=2,'col_1'=8] {'row_0','row_1'..., dimensions={0} | all-to-all | bytes 524288 | tf_op jit(solution)/shard_map/all_to_all | solution.py:207
  69.9 0.8 %reduce_sum.9 = f32[2,128]{1,0:T(2,128)} reduce(f32[256,2,128]{2,1,0:T(2,128)S(1)} %all_to_all.11, f32[]{:T(128)} %constant.3.clone.1), dimensions={0}, to_apply=%region_0.0 | reduce | flops 65280 | bytes 263172 | tf_op jit(solution)/shard_map/reduce_sum | solution.py:208

commit v2 on v1

--- a/solution.py
+++ b/solution.py
@@ -172,6 +172,7 @@
     return pl.pallas_call(
         depth_kernel,
         out_shape=jax.ShapeDtypeStruct((field.shape[1] // 2 * 4, rows // 2), F32),
+        compiler_params=pltpu.CompilerParams(vmem_limit_bytes=12 << 20),
         name="depth",
     )(field, tables)
 
@@ -185,6 +186,7 @@
             jax.ShapeDtypeStruct((devices * 2, 128), F32),
         ),
         scratch_shapes=[pltpu.VMEM((2 * SHELLS, 256), F32)],
+        compiler_params=pltpu.CompilerParams(vmem_limit_bytes=16 << 20),
         name="plane",
     )(recv, square, twiddle, shell)
 

time: 71 us -> 67.9 us (0.956)
  Pallas kernels: 10.4 us -> 6.55 us
  local copies, waits for them, and re-layouts: 0 us -> 2.09 us
  blocking collectives: 58.9 us -> 57.5 us
    unnamed x0 -> x10, local copies, waits for them, and re-layouts: none -> 2.09 us
    pallas_call x1, Pallas kernels: 2.45 us -> 0.43 us  [depth_call(): pl.pallas_call(depth_kernel, out_shape=jax.ShapeDtypeStruct((field.shape[...]
    pallas_call x1, Pallas kernels: 8 us -> 6.13 us  [plane_call(): pl.pallas_call(functools.partial(plane_kernel, scale, unit), out_shape=(j...]
    all_to_all x1, blocking collectives: 21.9 us -> 20.9 us  [local(): lax.all_to_all(sums.reshape(devices, 2, 128), ROW_COL, 0, 0, tiled=True)]
where the time goes in v2:
time: 67.9 us; the launch traced here: 67.7 us
  blocking collectives  57.5 us (85%)
  Pallas kernels  6.55 us (10%)
  local copies, waits for them, and re-layouts  2.09 us (3%)
  other arithmetic  0.84 us (1%)
    all_to_all x1, blocking collectives, local(): got = lax.all_to_all(sent, ROW_COL, 0, 0, tiled=True)  36.6 us
    all_to_all x1, blocking collectives, local(): lax.all_to_all(sums.reshape(devices, 2, 128), ROW_COL, 0, 0, tiled=True)  20.9 us
    pallas_call x1, Pallas kernels, plane_call(): pl.pallas_call(functools.partial(plane_kernel, scale, unit), out_shape=(j...  6.13 us
    unnamed x10, local copies, waits for them, and re-layouts  2.09 us

profile of v2, /device:TPU:1, one launch (start us, length us, event | category | flops | bytes accessed | tf_op | source)
XLA Modules:
  0.0 67.7 jit_solution(5055001232728388552)
XLA Ops:
  0.6 0.0 copy-start
  0.6 1.0 %copy-done = f32[1,16,16,512]{3,2,1,0:T(8,128)S(1)} copy-done((f32[1,16,16,512]{3,2,1,0:T(8,128)S(1)}, f32[1,16,16,512]{3,2,1,0:T(8,128)}, u32[]{:S(2)}) %copy-start) | copy-done | bytes 524312
  1.7 0.0 copy-start.3
  1.7 1.0 %copy-done.3 = bf16[2,2,256,256]{3,2,1,0:T(8,128)(2,1)S(1)} copy-done((bf16[2,2,256,256]{3,2,1,0:T(8,128)(2,1)S(1)}, bf16[2,2,256,256]{3,2,1,0:T(8,128)(2,1)}, u32[]{:S(2)}) %copy-start.3) | copy-done | bytes 524312
  2.7 0.0 copy-start.4
  2.7 0.4 depth.1
  3.2 0.0 copy-start.1
  3.2 0.0 copy-start.2
  3.2 36.6 %all_to_all.10 = f32[256,4,128]{2,1,0:T(4,128)S(1)} all-to-all(f32[256,4,128]{2,1,0:T(4,128)S(1)} %bitcast.8), channel_id=1, replica_groups=mesh['row_0'=4,'row_1'=2,'row_2'=2,'col_0'=2,'col_1'=8] {'row_0','row_1'..., dimensions={0} | all-to-all | bytes 1048576 | tf_op jit(solution)/shard_map/all_to_all | solution.py:205
  39.8 0.0 copy-done.4
  39.8 0.0 copy-done.1
  39.8 0.0 copy-done.2
  39.8 6.1 %plane.1 = (f32[256,256]{1,0:T(8,128)}, f32[512,128]{1,0:T(8,128)S(1)}) custom-call(f32[1024,128]{1,0:T(8,128)S(1)} %bitcast.7, bf16[2,2,256,256]{3,2,1,0:T(8,128)(2,1)S(1)} %copy-done.2, f32[2,256,256]{2,1,0:T(8,128)S(1)} %copy-done.1, s32[256,256]{1,0:T(8,128)S(1)} %bitcast.10), custom_call_target="tpu_custom_call" | custom-call | tf_op jit(solution)/shard_map/plane/pallas_call | solution.py:182
  45.9 20.9 %all_to_all.11 = f32[256,2,128]{2,1,0:T(2,128)S(1)} all-to-all(f32[256,2,128]{2,1,0:T(2,128)S(1)} %bitcast.11), channel_id=1, replica_groups=mesh['row_0'=4,'row_1'=2,'row_2'=2,'col_0'=2,'col_1'=8] {'row_0','row_1'..., dimensions={0} | all-to-all | bytes 524288 | tf_op jit(solution)/shard_map/all_to_all | solution.py:209
  66.9 0.8 %reduce_sum.9 = f32[2,128]{1,0:T(2,128)} reduce(f32[256,2,128]{2,1,0:T(2,128)S(1)} %all_to_all.11, f32[]{:T(128)} %constant.3.clone.1), dimensions={0}, to_apply=%region_0.0 | reduce | flops 65280 | bytes 263172 | tf_op jit(solution)/shard_map/reduce_sum | solution.py:210
Async XLA Ops:
  0.6 1.0 %copy-start = (f32[1,16,16,512]{3,2,1,0:T(8,128)S(1)}, f32[1,16,16,512]{3,2,1,0:T(8,128)}, u32[]{:S(2)}) copy-start(f32[1,16,16,512]{3,2,1,0:T(8,128)} %param.5) | copy-start | bytes 1572868
  1.7 1.0 %copy-start.3 = (bf16[2,2,256,256]{3,2,1,0:T(8,128)(2,1)S(1)}, bf16[2,2,256,256]{3,2,1,0:T(8,128)(2,1)}, u32[]{:S(2)}) copy-start(bf16[2,2,256,256]{3,2,1,0:T(8,128)(2,1)} %constant.8.clone.table_ref) | copy-start | bytes 1572868
  2.7 37.1 %copy-start.4 = (s32[1,256,256]{2,1,0:T(8,128)S(1)}, s32[1,256,256]{2,1,0:T(8,128)}, u32[]{:S(2)}) copy-start(s32[1,256,256]{2,1,0:T(8,128)} %param.6) | copy-start | bytes 786436
  3.2 36.7 %copy-start.1 = (f32[2,256,256]{2,1,0:T(8,128)S(1)}, f32[2,256,256]{2,1,0:T(8,128)}, u32[]{:S(2)}) copy-start(f32[2,256,256]{2,1,0:T(8,128)} %constant.10.clone.twiddle_ref) | copy-start | bytes 1572868
  3.2 36.7 %copy-start.2 = (bf16[2,2,256,256]{3,2,1,0:T(8,128)(2,1)S(1)}, bf16[2,2,256,256]{3,2,1,0:T(8,128)(2,1)}, u32[]{:S(2)}) copy-start(bf16[2,2,256,256]{3,2,1,0:T(8,128)(2,1)} %constant.9.clone.square_ref) | copy-start | bytes 1572868

commit v3 on v2

--- a/solution.py
+++ b/solution.py
@@ -14,6 +14,8 @@
 ROW = ("row_0", "row_1", "row_2")
 COL = ("col_0", "col_1")
 ROW_COL = ROW + COL
+CORE = "row_2"
+CHIPS = ("row_0", "row_1", "col_0", "col_1")
 F32 = jnp.float32
 BF16 = jnp.bfloat16
 
@@ -64,7 +66,15 @@
     return dot(lhs[0], rhs[0]) + dot(lhs[0], rhs[1]) + dot(lhs[1], rhs[0])
 
 
-def depth_kernel(field_ref, table_ref, out_ref):
+def depth_kernel(field_hbm, table_hbm, out_ref, field_ref, table_ref, sems):
+    copies = [
+        pltpu.make_async_copy(field_hbm, field_ref, sems.at[0]),
+        pltpu.make_async_copy(table_hbm, table_ref, sems.at[1]),
+    ]
+    for copy in copies:
+        copy.start()
+    for copy in copies:
+        copy.wait()
     half = field_ref.shape[1] // 2
     lanes = field_ref.shape[0] // 2
     freqs = table_ref.shape[2] // 2
@@ -97,7 +107,9 @@
     return blocks
 
 
-def plane_kernel(scale, unit, recv_ref, square_ref, twiddle_ref, shell_ref, power_ref, sums_ref, acc_ref):
+def plane_kernel(
+    scale, unit, recv_ref, square_ref, twiddle_ref, shell_ref, power_hbm, sums_ref, power_ref, sem
+):
     n = power_ref.shape[0]
     radix = math.isqrt(n)
     parts = [
@@ -122,30 +134,37 @@
         ]
         for b, block in enumerate(swap_digits(blocks, radix)):
             power_ref[b * radix : (b + 1) * radix, side * half : (side + 1) * half] = block
-
-    acc_ref[...] = jnp.zeros_like(acc_ref)
-
-    def add_rows(index, carry):
-        rows = pl.ds(index * 16, 16)
+    copy = pltpu.make_async_copy(power_ref, power_hbm, sem)
+    copy.start()
+
+    picks = []
+    marked = []
+    for index in range(n // 16):
+        rows = slice(index * 16, (index + 1) * 16)
         upper, lower = split_two(power_ref[rows, :])
         marks = shell_ref[rows, :]
         high = (marks >> 4).astype(F32).astype(BF16)
         low = (marks & 15).astype(F32).astype(BF16)
         zero = jnp.zeros_like(upper)
         one = jnp.ones_like(upper)
-        picks = [jnp.where(high == jnp.array(h, BF16), upper, zero) for h in range(16)]
-        picks += [jnp.where(high == jnp.array(h, BF16), lower, zero) for h in range(16)]
-        marked = [jnp.where(low == jnp.array(l, BF16), one, zero) for l in range(16)]
-        acc_ref[...] += lax.dot_general(
-            jnp.concatenate(picks, axis=0),
-            jnp.concatenate(marked, axis=0),
-            NT,
-            preferred_element_type=F32,
+        flags = [high == jnp.array(h, BF16) for h in range(16)]
+        picks.append(
+            jnp.concatenate(
+                [jnp.where(flag, piece, zero) for piece in (upper, lower) for flag in flags], axis=0
+            )
         )
-        return carry
-
-    lax.fori_loop(0, n // 16, add_rows, 0)
-    acc = acc_ref[:SHELLS, :] + acc_ref[SHELLS:, :]
+        marked.append(
+            jnp.concatenate(
+                [jnp.where(low == jnp.array(l, BF16), one, zero) for l in range(16)], axis=0
+            )
+        )
+    acc = lax.dot_general(
+        jnp.concatenate(picks, axis=1),
+        jnp.concatenate(marked, axis=1),
+        NT,
+        preferred_element_type=F32,
+    )
+    acc = acc[:SHELLS, :] + acc[SHELLS:, :]
     row = lax.broadcasted_iota(jnp.int32, (256, 256), 0)
     lane = lax.broadcasted_iota(jnp.int32, (256, 256), 1)
     same = jnp.where((row & 15) == (lane & 15), acc, 0.0)
@@ -162,31 +181,37 @@
     lane = lax.broadcasted_iota(jnp.int32, (16, 256), 1)
     sums = jnp.sum(jnp.where((lane >> 4) == row, wide, 0.0), axis=0, keepdims=True) * unit
     for side in range(2):
-        piece = sums[:, side * 128 : (side + 1) * 128]
-        count = sums_ref.shape[0] // 2
-        sums_ref[pl.ds(side, count, stride=2), :] = jnp.broadcast_to(piece, (count, 128))
+        sums_ref[side : side + 1, :] = sums[:, side * 128 : (side + 1) * 128]
+    copy.wait()
 
 
 def depth_call(field, tables):
     rows = field.shape[0]
     return pl.pallas_call(
         depth_kernel,
+        in_specs=[pl.BlockSpec(memory_space=pltpu.HBM)] * 2,
         out_shape=jax.ShapeDtypeStruct((field.shape[1] // 2 * 4, rows // 2), F32),
+        scratch_shapes=[
+            pltpu.VMEM(field.shape, field.dtype),
+            pltpu.VMEM(tables.shape, tables.dtype),
+            pltpu.SemaphoreType.DMA((2,)),
+        ],
         compiler_params=pltpu.CompilerParams(vmem_limit_bytes=12 << 20),
         name="depth",
     )(field, tables)
 
 
-def plane_call(recv, square, twiddle, shell, devices, scale, unit):
+def plane_call(recv, square, twiddle, shell, scale, unit):
     n = shell.shape[0]
     return pl.pallas_call(
         functools.partial(plane_kernel, scale, unit),
         out_shape=(
             jax.ShapeDtypeStruct((n, n), F32),
-            jax.ShapeDtypeStruct((devices * 2, 128), F32),
+            jax.ShapeDtypeStruct((2, 128), F32),
         ),
-        scratch_shapes=[pltpu.VMEM((2 * SHELLS, 256), F32)],
-        compiler_params=pltpu.CompilerParams(vmem_limit_bytes=16 << 20),
+        out_specs=(pl.BlockSpec(memory_space=pltpu.HBM), pl.BlockSpec(memory_space=pltpu.VMEM)),
+        scratch_shapes=[pltpu.VMEM((n, n), F32), pltpu.SemaphoreType.DMA],
+        compiler_params=pltpu.CompilerParams(vmem_limit_bytes=24 << 20),
         name="plane",
     )(recv, square, twiddle, shell)
 
@@ -204,9 +229,12 @@
     sent = sent.reshape(devices, 4, 128)
     got = lax.all_to_all(sent, ROW_COL, 0, 0, tiled=True)
     power, sums = plane_call(
-        got.reshape(devices * 4, 128), square, twiddle, shell.reshape(ny, nx), devices, scale, unit
+        got.reshape(devices * 4, 128), square, twiddle, shell.reshape(ny, nx), scale, unit
     )
-    sums = lax.all_to_all(sums.reshape(devices, 2, 128), ROW_COL, 0, 0, tiled=True)
+    sums = sums + lax.ppermute(sums, CORE, [(0, 1), (1, 0)])
+    chips = devices // lax.axis_size(CORE)
+    sums = jnp.broadcast_to(sums, (chips, 2, 128))
+    sums = lax.all_to_all(sums, CHIPS, 0, 0, tiled=True)
     spectrum = jnp.sum(sums, axis=0).reshape(fields, SHELLS)
     return (power.reshape(fields, 1, ny, nx), spectrum)
 

time: 67.9 us -> 63.1 us (0.929)
  blocking collectives: 57.5 us -> 53.9 us
  Pallas kernels: 6.55 us -> 3.97 us
  waiting for transfers between devices: 0 us -> 0.82 us
    all_to_all x1, blocking collectives: 20.9 us -> 17.3 us  [local(): sums = lax.all_to_all(sums, CHIPS, 0, 0, tiled=True)]
    pallas_call x1, Pallas kernels: 6.13 us -> 3.45 us  [plane_call(): pl.pallas_call(functools.partial(plane_kernel, scale, unit), out_shape=(j...]
    ppermute x0 -> x1, waiting for transfers between devices: none -> 0.82 us  [local(): sums = sums + lax.ppermute(sums, CORE, [(0, 1), (1, 0)])]
  transfers between devices with their start and end apart: 0 -> 1, of which waited for: 0 -> 1; matrix products, arithmetic and copies ran while one was open for 0% -> 0% of each run, Pallas kernels for 0% -> 0%
where the time goes in v3:
time: 63.1 us; the launch traced here: 62.9 us
  blocking collectives  53.9 us (85%)
  Pallas kernels  3.97 us (6%)
  local copies, waits for them, and re-layouts  2.13 us (3%)
  waiting for transfers between devices  0.82 us (1%)
  other arithmetic  0.71 us (1%)
  between operations  0.68 us (1%)
  starting transfers between devices  0.64 us (1%)
    all_to_all x1, blocking collectives, local(): got = lax.all_to_all(sent, ROW_COL, 0, 0, tiled=True)  36.6 us
    all_to_all x1, blocking collectives, local(): sums = lax.all_to_all(sums, CHIPS, 0, 0, tiled=True)  17.3 us
    pallas_call x1, Pallas kernels, plane_call(): pl.pallas_call(functools.partial(plane_kernel, scale, unit), out_shape=(j...  3.45 us
    unnamed x10, local copies, waits for them, and re-layouts  2.09 us
  transfers between devices with their start and end apart: 1, of which 1 were waited for; matrix products, arithmetic and copies ran while one was open for 0% of the time, Pallas kernels for 0%

profile of v3, /device:TPU:1, one launch (start us, length us, event | category | flops | bytes accessed | tf_op | source)
XLA Modules:
  0.0 62.9 jit_solution(11362086072085414)
XLA Ops:
  0.6 0.0 copy-start
  0.6 1.0 %copy-done = f32[1,16,16,512]{3,2,1,0:T(8,128)S(1)} copy-done((f32[1,16,16,512]{3,2,1,0:T(8,128)S(1)}, f32[1,16,16,512]{3,2,1,0:T(8,128)}, u32[]{:S(2)}) %copy-start) | copy-done | bytes 524312
  1.7 0.0 copy-start.3
  1.7 1.0 %copy-done.3 = bf16[2,2,256,256]{3,2,1,0:T(8,128)(2,1)S(1)} copy-done((bf16[2,2,256,256]{3,2,1,0:T(8,128)(2,1)S(1)}, bf16[2,2,256,256]{3,2,1,0:T(8,128)(2,1)}, u32[]{:S(2)}) %copy-start.3) | copy-done | bytes 524312
  2.7 0.0 copy-start.4
  2.7 0.5 depth.1
  3.2 0.0 copy-start.1
  3.3 0.0 copy-start.2
  3.3 36.6 %all_to_all.10 = f32[256,4,128]{2,1,0:T(4,128)S(1)} all-to-all(f32[256,4,128]{2,1,0:T(4,128)S(1)} %bitcast.7), channel_id=1, replica_groups=mesh['row_0'=4,'row_1'=2,'row_2'=2,'col_0'=2,'col_1'=8] {'row_0','row_1'..., dimensions={0} | all-to-all | bytes 1048576 | tf_op jit(solution)/shard_map/all_to_all | solution.py:230
  39.9 0.0 copy-done.4
  39.9 0.0 copy-done.1
  39.9 0.0 copy-done.2
  39.9 3.4 %plane.1 = (f32[256,256]{1,0:T(8,128)}, f32[2,128]{1,0:T(2,128)S(1)}) custom-call(f32[1024,128]{1,0:T(8,128)S(1)} %bitcast.6, bf16[2,2,256,256]{3,2,1,0:T(8,128)(2,1)S(1)} %copy-done.2, f32[2,256,256]{2,1,0:T(8,128)S(1)} %copy-done.1, s32[256,256]{1,0:T(8,128)S(1)} %bitcast.9), custom_call_target="tpu_custom_call" | custom-call | tf_op jit(solution)/shard_map/plane/pallas_call | solution.py:206
  43.4 0.6 %collective-permute-start = (f32[2,128]{1,0:T(2,128)S(1)}, f32[2,128]{1,0:T(2,128)S(1)}, u32[]{:S(2)}, u32[]{:S(2)}) collective-permute-start(f32[2,128]{1,0:T(2,128)S(1)} %get-tuple-element.5), channel_id=1, source_target_pairs={{0,16},{16,0},{1,17},{17,1},{2,18},{18,2},{3,19},{19,3},{4,20},{20... | collective-permute-start | bytes 3080 | tf_op jit(solution)/shard_map/ppermute | solution.py:234
  44.0 0.8 %collective-permute-done = f32[2,128]{1,0:T(2,128)S(1)} collective-permute-done((f32[2,128]{1,0:T(2,128)S(1)}, f32[2,128]{1,0:T(2,128)S(1)}, u32[]{:S(2)}, u32[]{:S(2)}) %collective-permute-start) | collective-permute-done | bytes 1056 | tf_op jit(solution)/shard_map/ppermute | solution.py:234
  44.9 17.3 %all_to_all.11 = f32[128,2,128]{2,1,0:T(2,128)S(1)} all-to-all(f32[128,2,128]{2,1,0:T(2,128)S(1)} %broadcast_in_dim.3), channel_id=1, replica_groups=mesh['row_0'=4,'row_1'=2,'row_2'=2,'col_0'=2,'col_1'=8] {'row_0','row_1'..., dimensions={0} | all-to-all | bytes 262144 | tf_op jit(solution)/shard_map/all_to_all | solution.py:237
  62.1 0.7 %reduce_sum.9 = f32[2,128]{1,0:T(2,128)} reduce(f32[128,2,128]{2,1,0:T(2,128)S(1)} %all_to_all.11, f32[]{:T(128)} %constant.3.clone.1), dimensions={0}, to_apply=%region_0.0 | reduce | flops 32512 | bytes 132100 | tf_op jit(solution)/shard_map/reduce_sum | solution.py:238
  (2 shorter events, 0.0 us)
Async XLA Ops:
  0.6 1.0 %copy-start = (f32[1,16,16,512]{3,2,1,0:T(8,128)S(1)}, f32[1,16,16,512]{3,2,1,0:T(8,128)}, u32[]{:S(2)}) copy-start(f32[1,16,16,512]{3,2,1,0:T(8,128)} %param.5) | copy-start | bytes 1572868
  1.7 1.0 %copy-start.3 = (bf16[2,2,256,256]{3,2,1,0:T(8,128)(2,1)S(1)}, bf16[2,2,256,256]{3,2,1,0:T(8,128)(2,1)}, u32[]{:S(2)}) copy-start(bf16[2,2,256,256]{3,2,1,0:T(8,128)(2,1)} %constant.8.clone.table_hbm) | copy-start | bytes 1572868
  2.7 37.2 %copy-start.4 = (s32[1,256,256]{2,1,0:T(8,128)S(1)}, s32[1,256,256]{2,1,0:T(8,128)}, u32[]{:S(2)}) copy-start(s32[1,256,256]{2,1,0:T(8,128)} %param.6) | copy-start | bytes 786436
  3.2 36.7 %copy-start.1 = (f32[2,256,256]{2,1,0:T(8,128)S(1)}, f32[2,256,256]{2,1,0:T(8,128)}, u32[]{:S(2)}) copy-start(f32[2,256,256]{2,1,0:T(8,128)} %constant.10.clone.twiddle_ref) | copy-start | bytes 1572868
  3.3 36.7 %copy-start.2 = (bf16[2,2,256,256]{3,2,1,0:T(8,128)(2,1)S(1)}, bf16[2,2,256,256]{3,2,1,0:T(8,128)(2,1)}, u32[]{:S(2)}) copy-start(bf16[2,2,256,256]{3,2,1,0:T(8,128)(2,1)} %constant.9.clone.square_ref) | copy-start | bytes 1572868
  43.4 1.5 %collective-permute-start = (f32[2,128]{1,0:T(2,128)S(1)}, f32[2,128]{1,0:T(2,128)S(1)}, u32[]{:S(2)}, u32[]{:S(2)}) collective-permute-start(f32[2,128]{1,0:T(2,128)S(1)} %get-tuple-element.5), channel_id=1, source_target_pairs={{0,16},{16,0},{1,17},{17,1},{2,18},{18,2},{3,19},{19,3},{4,20},{20... | collective-permute-start | bytes 3080 | tf_op jit(solution)/shard_map/ppermute | solution.py:234

commit v4 on v3

--- a/solution.py
+++ b/solution.py
@@ -44,12 +44,20 @@
     n = np.arange(radix)
     base = np.multiply.outer(n, n)
     both = base[:, None, :, None] + base[None, :, None, :]
-    both = both.reshape(radix * radix, radix * radix)
-    angle = 2.0 * math.pi / radix * (both % radix)
-    square = np.stack([split_table(np.cos(angle)), split_table(-np.sin(angle))])
-    angle = 2.0 * math.pi / (radix * radix) * (both % (radix * radix))
+    split = (radix, 2, radix // 2, radix * radix)
+    size = (radix * radix, radix * radix)
+    ordered = both.reshape(split).transpose(1, 0, 2, 3).reshape(size)
+    both = both.reshape(size)
+    unit = 2.0 * math.pi / radix
+    left = np.stack([split_table(f(unit * (ordered % radix))) for f in (np.cos, minus_sin)])
+    right = np.stack([split_table(f(unit * (both % radix))) for f in (np.cos, minus_sin)])
+    angle = unit / radix * ordered
     twiddle = np.stack([np.cos(angle), -np.sin(angle)]).astype(np.float32)
-    return square, twiddle
+    return left, right, twiddle
+
+
+def minus_sin(angle):
+    return -np.sin(angle)
 
 
 def split_two(values):
@@ -108,78 +116,84 @@
 
 
 def plane_kernel(
-    scale, unit, recv_ref, square_ref, twiddle_ref, shell_ref, power_hbm, sums_ref, power_ref, sem
+    scale,
+    unit,
+    recv_ref,
+    left_ref,
+    right_ref,
+    twiddle_ref,
+    shell_ref,
+    power_hbm,
+    sums_ref,
+    power_ref,
+    sem,
 ):
     n = power_ref.shape[0]
     radix = math.isqrt(n)
+    half = n // 2
+    low_rows = radix // 2
+    dot = functools.partial(lax.dot_general, preferred_element_type=F32)
     parts = [
         jnp.concatenate([recv_ref[pl.ds(2 * c + s, n, stride=4), :] for s in range(2)], axis=1)
         for c in range(2)
     ]
     re, im = split_two(parts[0]), split_two(parts[1])
-    cos = (square_ref[0, 0], square_ref[0, 1])
-    sin = (square_ref[1, 0], square_ref[1, 1])
-    u_re = dot3(cos, re, NN) - dot3(sin, im, NN)
-    u_im = dot3(sin, re, NN) + dot3(cos, im, NN)
-    t_re, t_im = twiddle_ref[0], twiddle_ref[1]
-    re = split_two(u_re * t_re - u_im * t_im)
-    im = split_two(u_re * t_im + u_im * t_re)
-    v_re = dot3(re, cos, NN) - dot3(im, sin, NN)
-    v_im = dot3(re, sin, NN) + dot3(im, cos, NN)
-    power = (v_re * v_re + v_im * v_im) * scale
-    half = n // 2
-    for side in range(2):
-        blocks = [
-            power[a * radix : (a + 1) * radix, side * half : (side + 1) * half] for a in range(radix)
-        ]
-        for b, block in enumerate(swap_digits(blocks, radix)):
-            power_ref[b * radix : (b + 1) * radix, side * half : (side + 1) * half] = block
+    cos, sin = (left_ref[0, 0], left_ref[0, 1]), (left_ref[1, 0], left_ref[1, 1])
+    to_re = jnp.concatenate([cos[0], -sin[0], cos[0], -sin[0], cos[1], -sin[1]], axis=1)
+    to_im = jnp.concatenate([sin[0], cos[0], sin[0], cos[0], sin[1], cos[1]], axis=1)
+    moved = jnp.concatenate([re[0], im[0], re[1], im[1], re[0], im[0]], axis=0)
+    first = dot(jnp.concatenate([to_re, to_im], axis=0), moved, NN)
+    cos, sin = (right_ref[0, 0], right_ref[0, 1]), (right_ref[1, 0], right_ref[1, 1])
+    to_re = jnp.concatenate([cos[0], -sin[0], cos[0], -sin[0], cos[1], -sin[1]], axis=0)
+    to_im = jnp.concatenate([sin[0], cos[0], sin[0], cos[0], sin[1], cos[1]], axis=0)
+
+    picks = []
+    marked = []
+    for part in range(2):
+        rows = slice(part * half, (part + 1) * half)
+        u_re, u_im = first[rows, :], first[n + part * half : n + (part + 1) * half, :]
+        t_re, t_im = twiddle_ref[0, rows, :], twiddle_ref[1, rows, :]
+        re = split_two(u_re * t_re - u_im * t_im)
+        im = split_two(u_re * t_im + u_im * t_re)
+        turned = jnp.concatenate([re[0], im[0], re[1], im[1], re[0], im[0]], axis=1)
+        v_re = dot(turned, to_re, NN)
+        v_im = dot(turned, to_im, NN)
+        power = (v_re * v_re + v_im * v_im) * scale
+        sides = []
+        for side in range(2):
+            lanes = slice(side * half, (side + 1) * half)
+            blocks = [power[a * low_rows : (a + 1) * low_rows, lanes] for a in range(radix)]
+            sides.append(swap_digits(blocks, radix))
+        tiles = [jnp.concatenate([sides[0][b], sides[1][b]], axis=1) for b in range(radix)]
+        spots = [slice(b * radix + part * low_rows, b * radix + (part + 1) * low_rows) for b in range(radix)]
+        for spot, tile in zip(spots, tiles):
+            power_ref[spot, :] = tile
+        for b in range(0, radix, 2):
+            upper, lower = split_two(jnp.concatenate(tiles[b : b + 2], axis=0))
+            marks = jnp.concatenate([shell_ref[spot, :] for spot in spots[b : b + 2]], axis=0)
+            high = (marks >> 4).astype(F32).astype(BF16)
+            low = (marks & 15).astype(F32).astype(BF16)
+            zero = jnp.zeros_like(upper)
+            one = jnp.ones_like(upper)
+            flags = [high == jnp.array(h, BF16) for h in range(16)]
+            picked = [jnp.where(flag, piece, zero) for piece in (upper, lower) for flag in flags]
+            picks.append(jnp.concatenate(picked, axis=0))
+            flags = [low == jnp.array(l, BF16) for l in range(16)]
+            marked.append(jnp.concatenate([jnp.where(flag, one, zero) for flag in flags], axis=0))
     copy = pltpu.make_async_copy(power_ref, power_hbm, sem)
     copy.start()
-
-    picks = []
-    marked = []
-    for index in range(n // 16):
-        rows = slice(index * 16, (index + 1) * 16)
-        upper, lower = split_two(power_ref[rows, :])
-        marks = shell_ref[rows, :]
-        high = (marks >> 4).astype(F32).astype(BF16)
-        low = (marks & 15).astype(F32).astype(BF16)
-        zero = jnp.zeros_like(upper)
-        one = jnp.ones_like(upper)
-        flags = [high == jnp.array(h, BF16) for h in range(16)]
-        picks.append(
-            jnp.concatenate(
-                [jnp.where(flag, piece, zero) for piece in (upper, lower) for flag in flags], axis=0
-            )
-        )
-        marked.append(
-            jnp.concatenate(
-                [jnp.where(low == jnp.array(l, BF16), one, zero) for l in range(16)], axis=0
-            )
-        )
-    acc = lax.dot_general(
-        jnp.concatenate(picks, axis=1),
-        jnp.concatenate(marked, axis=1),
-        NT,
-        preferred_element_type=F32,
-    )
+    acc = dot(jnp.concatenate(picks, axis=1), jnp.concatenate(marked, axis=1), NT)
     acc = acc[:SHELLS, :] + acc[SHELLS:, :]
     row = lax.broadcasted_iota(jnp.int32, (256, 256), 0)
     lane = lax.broadcasted_iota(jnp.int32, (256, 256), 1)
-    same = jnp.where((row & 15) == (lane & 15), acc, 0.0)
-    by_high = jnp.sum(same.reshape(16, 16, 256), axis=1)
+    same = jnp.where((row & 15) == (lane & 15), acc, 0.0).reshape(16, 16, 256)
+    by_high = (same[:, :8, :] + same[:, 8:, :]).reshape(128, 256)
     spread = ((row >> 4) == (lane & 15)).astype(F32).astype(BF16)
-    upper = by_high.astype(BF16)
-    rest = by_high - upper.astype(F32)
-    middle, lower = split_two(rest)
-    wide = sum(
-        lax.dot_general(piece, spread, NN, preferred_element_type=F32)
-        for piece in (upper, middle, lower)
-    )
-    row = lax.broadcasted_iota(jnp.int32, (16, 256), 0)
-    lane = lax.broadcasted_iota(jnp.int32, (16, 256), 1)
-    sums = jnp.sum(jnp.where((lane >> 4) == row, wide, 0.0), axis=0, keepdims=True) * unit
+    upper, lower = split_two(by_high)
+    wide = dot(upper, spread, NN) + dot(lower, spread, NN)
+    row = lax.broadcasted_iota(jnp.int32, (128, 256), 0)
+    lane = lax.broadcasted_iota(jnp.int32, (128, 256), 1)
+    sums = jnp.sum(jnp.where((lane >> 4) == (row >> 3), wide, 0.0), axis=0, keepdims=True) * unit
     for side in range(2):
         sums_ref[side : side + 1, :] = sums[:, side * 128 : (side + 1) * 128]
     copy.wait()
@@ -187,6 +201,8 @@
 
 def depth_call(field, tables):
     rows = field.shape[0]
+    field = pltpu.with_memory_space_constraint(field, pltpu.HBM)
+    tables = pltpu.with_memory_space_constraint(tables, pltpu.HBM)
     return pl.pallas_call(
         depth_kernel,
         in_specs=[pl.BlockSpec(memory_space=pltpu.HBM)] * 2,
@@ -201,7 +217,7 @@
     )(field, tables)
 
 
-def plane_call(recv, square, twiddle, shell, scale, unit):
+def plane_call(recv, left, right, twiddle, shell, scale, unit):
     n = shell.shape[0]
     return pl.pallas_call(
         functools.partial(plane_kernel, scale, unit),
@@ -213,7 +229,7 @@
         scratch_shapes=[pltpu.VMEM((n, n), F32), pltpu.SemaphoreType.DMA],
         compiler_params=pltpu.CompilerParams(vmem_limit_bytes=24 << 20),
         name="plane",
-    )(recv, square, twiddle, shell)
+    )(recv, left, right, twiddle, shell)
 
 
 def local(field, shell):
@@ -222,15 +238,14 @@
     n_col = lax.axis_size(COL)
     devices = n_row * n_col
     nx, ny, keep = cx * n_row, cy * n_col, nz // 2
-    square, twiddle = plane_tables(n_row)
+    left, right, twiddle = plane_tables(n_row)
     scale = 1.0 / (float(nx) * ny * nz)
     unit = float(SHELLS) / (keep * ny * nx)
-    sent = depth_call(field.reshape(cx * cy, nz), depth_tables(nz))
+    sent = depth_call(field.reshape(cx * cy, nz), jnp.asarray(depth_tables(nz)))
     sent = sent.reshape(devices, 4, 128)
     got = lax.all_to_all(sent, ROW_COL, 0, 0, tiled=True)
-    power, sums = plane_call(
-        got.reshape(devices * 4, 128), square, twiddle, shell.reshape(ny, nx), scale, unit
-    )
+    got = got.reshape(devices * 4, 128)
+    power, sums = plane_call(got, left, right, twiddle, shell.reshape(ny, nx), scale, unit)
     sums = sums + lax.ppermute(sums, CORE, [(0, 1), (1, 0)])
     chips = devices // lax.axis_size(CORE)
     sums = jnp.broadcast_to(sums, (chips, 2, 128))

time: 63.1 us -> 62.5 us (level)
  local copies, waits for them, and re-layouts: 2.13 us -> 0.06 us
  Pallas kernels: 3.97 us -> 5.51 us
    unnamed x10 -> x8, local copies, waits for them, and re-layouts: 2.09 us -> 0.02 us
    pallas_call x1, Pallas kernels: 0.52 us -> 1.72 us  [depth_call(): pl.pallas_call(depth_kernel, in_specs=[pl.BlockSpec(memory_space=pltpu.HB...]
where the time goes in v4:
time: 62.5 us; the launch traced here: 62.3 us
  blocking collectives  53.9 us (86%)
  Pallas kernels  5.51 us (9%)
  waiting for transfers between devices  0.82 us (1%)
  other arithmetic  0.71 us (1%)
  between operations  0.69 us (1%)
  starting transfers between devices  0.64 us (1%)
    all_to_all x1, blocking collectives, local(): got = lax.all_to_all(sent, ROW_COL, 0, 0, tiled=True)  36.6 us
    all_to_all x1, blocking collectives, local(): sums = lax.all_to_all(sums, CHIPS, 0, 0, tiled=True)  17.3 us
    pallas_call x1, Pallas kernels, plane_call(): pl.pallas_call(functools.partial(plane_kernel, scale, unit), out_shape=(j...  3.79 us
    pallas_call x1, Pallas kernels, depth_call(): pl.pallas_call(depth_kernel, in_specs=[pl.BlockSpec(memory_space=pltpu.HB...  1.72 us
  transfers between devices with their start and end apart: 1, of which 1 were waited for; matrix products, arithmetic and copies ran while one was open for 0% of the time, Pallas kernels for 0%

profile of v4, /device:TPU:1, one launch (start us, length us, event | category | flops | bytes accessed | tf_op | source)
XLA Modules:
  0.0 62.3 jit_solution(8297631878526776031)
XLA Ops:
  0.6 0.0 copy-start.2
  0.6 0.0 copy-start.3
  0.7 1.7 %depth.1 = f32[1024,128]{1,0:T(8,128)S(1)} custom-call(f32[256,512]{1,0:T(8,128)} %bitcast.9, bf16[2,2,256,256]{3,2,1,0:T(8,128)(2,1)} %constant.10.clone.table_hbm), custom_call_target="tpu_custom_call" | custom-call | tf_op jit(solution)/shard_map/depth/pallas_call | solution.py:206
  2.4 0.0 copy-start
  2.4 0.0 copy-start.1
  2.4 36.6 %all_to_all.10 = f32[256,4,128]{2,1,0:T(4,128)S(1)} all-to-all(f32[256,4,128]{2,1,0:T(4,128)S(1)} %bitcast.6), channel_id=1, replica_groups=mesh['row_0'=4,'row_1'=2,'row_2'=2,'col_0'=2,'col_1'=8] {'row_0','row_1'..., dimensions={0} | all-to-all | bytes 1048576 | tf_op jit(solution)/shard_map/all_to_all | solution.py:246
  39.0 0.0 copy-done.2
  39.0 0.0 copy-done.3
  39.0 0.0 copy-done
  39.0 0.0 copy-done.1
  39.1 3.8 %plane.1 = (f32[256,256]{1,0:T(8,128)}, f32[2,128]{1,0:T(2,128)S(1)}) custom-call(f32[1024,128]{1,0:T(8,128)S(1)} %bitcast.7, bf16[2,2,256,256]{3,2,1,0:T(8,128)(2,1)S(1)} %copy-done.2, bf16[2,2,256,256]{3,2,1,0:T(8,128)(2,1)S(1)} %copy-done.1, f32[2,256,256]{2,1,0:T(8,128)S(1)} %copy-done, s32[256,256]{1,0:T(8,128)S(1)} %bitcast.8), custom_call_target="tpu_custom_call" | custom-call | tf_op jit(solution)/shard_map/plane/pallas_call | solution.py:222
  42.9 0.6 %collective-permute-start = (f32[2,128]{1,0:T(2,128)S(1)}, f32[2,128]{1,0:T(2,128)S(1)}, u32[]{:S(2)}, u32[]{:S(2)}) collective-permute-start(f32[2,128]{1,0:T(2,128)S(1)} %get-tuple-element.5), channel_id=1, source_target_pairs={{0,16},{16,0},{1,17},{17,1},{2,18},{18,2},{3,19},{19,3},{4,20},{20... | collective-permute-start | bytes 3080 | tf_op jit(solution)/shard_map/ppermute | solution.py:249
  43.5 0.8 %collective-permute-done = f32[2,128]{1,0:T(2,128)S(1)} collective-permute-done((f32[2,128]{1,0:T(2,128)S(1)}, f32[2,128]{1,0:T(2,128)S(1)}, u32[]{:S(2)}, u32[]{:S(2)}) %collective-permute-start) | collective-permute-done | bytes 1056 | tf_op jit(solution)/shard_map/ppermute | solution.py:249
  44.4 17.3 %all_to_all.11 = f32[128,2,128]{2,1,0:T(2,128)S(1)} all-to-all(f32[128,2,128]{2,1,0:T(2,128)S(1)} %broadcast_in_dim.3), channel_id=1, replica_groups=mesh['row_0'=4,'row_1'=2,'row_2'=2,'col_0'=2,'col_1'=8] {'row_0','row_1'..., dimensions={0} | all-to-all | bytes 262144 | tf_op jit(solution)/shard_map/all_to_all | solution.py:252
  61.6 0.7 %reduce_sum.9 = f32[2,128]{1,0:T(2,128)} reduce(f32[128,2,128]{2,1,0:T(2,128)S(1)} %all_to_all.11, f32[]{:T(128)} %constant.4.clone.1), dimensions={0}, to_apply=%region_0.0 | reduce | flops 32512 | bytes 132100 | tf_op jit(solution)/shard_map/reduce_sum | solution.py:253
  (2 shorter events, 0.0 us)
Async XLA Ops:
  0.6 38.4 %copy-start.2 = (bf16[2,2,256,256]{3,2,1,0:T(8,128)(2,1)S(1)}, bf16[2,2,256,256]{3,2,1,0:T(8,128)(2,1)}, u32[]{:S(2)}) copy-start(bf16[2,2,256,256]{3,2,1,0:T(8,128)(2,1)} %constant.11.clone.left_ref) | copy-start | bytes 1572868
  0.6 38.4 %copy-start.3 = (s32[1,256,256]{2,1,0:T(8,128)S(1)}, s32[1,256,256]{2,1,0:T(8,128)}, u32[]{:S(2)}) copy-start(s32[1,256,256]{2,1,0:T(8,128)} %param.7) | copy-start | bytes 786436
  2.4 36.7 %copy-start = (f32[2,256,256]{2,1,0:T(8,128)S(1)}, f32[2,256,256]{2,1,0:T(8,128)}, u32[]{:S(2)}) copy-start(f32[2,256,256]{2,1,0:T(8,128)} %constant.13.clone.twiddle_ref) | copy-start | bytes 1572868
  2.4 36.7 %copy-start.1 = (bf16[2,2,256,256]{3,2,1,0:T(8,128)(2,1)S(1)}, bf16[2,2,256,256]{3,2,1,0:T(8,128)(2,1)}, u32[]{:S(2)}) copy-start(bf16[2,2,256,256]{3,2,1,0:T(8,128)(2,1)} %constant.12.clone.right_ref) | copy-start | bytes 1572868
  42.9 1.5 %collective-permute-start = (f32[2,128]{1,0:T(2,128)S(1)}, f32[2,128]{1,0:T(2,128)S(1)}, u32[]{:S(2)}, u32[]{:S(2)}) collective-permute-start(f32[2,128]{1,0:T(2,128)S(1)} %get-tuple-element.5), channel_id=1, source_target_pairs={{0,16},{16,0},{1,17},{17,1},{2,18},{18,2},{3,19},{19,3},{4,20},{20... | collective-permute-start | bytes 3080 | tf_op jit(solution)/shard_map/ppermute | solution.py:249

commit v5 on v3

--- a/solution.py
+++ b/solution.py
@@ -128,58 +128,41 @@
     v_im = dot3(re, sin, NN) + dot3(im, cos, NN)
     power = (v_re * v_re + v_im * v_im) * scale
     half = n // 2
+    picks = []
+    marked = []
     for side in range(2):
-        blocks = [
-            power[a * radix : (a + 1) * radix, side * half : (side + 1) * half] for a in range(radix)
-        ]
-        for b, block in enumerate(swap_digits(blocks, radix)):
-            power_ref[b * radix : (b + 1) * radix, side * half : (side + 1) * half] = block
+        lanes = slice(side * half, (side + 1) * half)
+        blocks = [power[a * radix : (a + 1) * radix, lanes] for a in range(radix)]
+        for index, tile in enumerate(swap_digits(blocks, radix)):
+            rows = slice(index * radix, (index + 1) * radix)
+            power_ref[rows, lanes] = tile
+            upper, lower = split_two(tile)
+            marks = shell_ref[rows, lanes]
+            high = (marks >> 4).astype(F32).astype(BF16)
+            low = (marks & 15).astype(F32).astype(BF16)
+            zero = jnp.zeros_like(upper)
+            one = jnp.ones_like(upper)
+            flags = [high == jnp.array(h, BF16) for h in range(16)]
+            picked = [jnp.where(flag, piece, zero) for piece in (upper, lower) for flag in flags]
+            picks.append(jnp.concatenate(picked, axis=0))
+            flags = [low == jnp.array(l, BF16) for l in range(16)]
+            picked = [jnp.where(flag, one, zero) for flag in flags]
+            marked.append(jnp.concatenate(picked, axis=0))
     copy = pltpu.make_async_copy(power_ref, power_hbm, sem)
     copy.start()
-
-    picks = []
-    marked = []
-    for index in range(n // 16):
-        rows = slice(index * 16, (index + 1) * 16)
-        upper, lower = split_two(power_ref[rows, :])
-        marks = shell_ref[rows, :]
-        high = (marks >> 4).astype(F32).astype(BF16)
-        low = (marks & 15).astype(F32).astype(BF16)
-        zero = jnp.zeros_like(upper)
-        one = jnp.ones_like(upper)
-        flags = [high == jnp.array(h, BF16) for h in range(16)]
-        picks.append(
-            jnp.concatenate(
-                [jnp.where(flag, piece, zero) for piece in (upper, lower) for flag in flags], axis=0
-            )
-        )
-        marked.append(
-            jnp.concatenate(
-                [jnp.where(low == jnp.array(l, BF16), one, zero) for l in range(16)], axis=0
-            )
-        )
-    acc = lax.dot_general(
-        jnp.concatenate(picks, axis=1),
-        jnp.concatenate(marked, axis=1),
-        NT,
-        preferred_element_type=F32,
-    )
+    dot = functools.partial(lax.dot_general, preferred_element_type=F32)
+    acc = dot(jnp.concatenate(picks, axis=1), jnp.concatenate(marked, axis=1), NT)
     acc = acc[:SHELLS, :] + acc[SHELLS:, :]
     row = lax.broadcasted_iota(jnp.int32, (256, 256), 0)
     lane = lax.broadcasted_iota(jnp.int32, (256, 256), 1)
-    same = jnp.where((row & 15) == (lane & 15), acc, 0.0)
-    by_high = jnp.sum(same.reshape(16, 16, 256), axis=1)
+    same = jnp.where((row & 15) == (lane & 15), acc, 0.0).reshape(16, 16, 256)
+    by_high = (same[:, :8, :] + same[:, 8:, :]).reshape(128, 256)
     spread = ((row >> 4) == (lane & 15)).astype(F32).astype(BF16)
-    upper = by_high.astype(BF16)
-    rest = by_high - upper.astype(F32)
-    middle, lower = split_two(rest)
-    wide = sum(
-        lax.dot_general(piece, spread, NN, preferred_element_type=F32)
-        for piece in (upper, middle, lower)
-    )
-    row = lax.broadcasted_iota(jnp.int32, (16, 256), 0)
-    lane = lax.broadcasted_iota(jnp.int32, (16, 256), 1)
-    sums = jnp.sum(jnp.where((lane >> 4) == row, wide, 0.0), axis=0, keepdims=True) * unit
+    upper, lower = split_two(by_high)
+    wide = dot(upper, spread, NN) + dot(lower, spread, NN)
+    row = lax.broadcasted_iota(jnp.int32, (128, 256), 0)
+    lane = lax.broadcasted_iota(jnp.int32, (128, 256), 1)
+    sums = jnp.sum(jnp.where((lane >> 4) == (row >> 3), wide, 0.0), axis=0, keepdims=True) * unit
     for side in range(2):
         sums_ref[side : side + 1, :] = sums[:, side * 128 : (side + 1) * 128]
     copy.wait()
@@ -187,6 +170,8 @@
 
 def depth_call(field, tables):
     rows = field.shape[0]
+    field = pltpu.with_memory_space_constraint(field, pltpu.HBM)
+    tables = pltpu.with_memory_space_constraint(tables, pltpu.HBM)
     return pl.pallas_call(
         depth_kernel,
         in_specs=[pl.BlockSpec(memory_space=pltpu.HBM)] * 2,
@@ -225,12 +210,11 @@
     square, twiddle = plane_tables(n_row)
     scale = 1.0 / (float(nx) * ny * nz)
     unit = float(SHELLS) / (keep * ny * nx)
-    sent = depth_call(field.reshape(cx * cy, nz), depth_tables(nz))
+    sent = depth_call(field.reshape(cx * cy, nz), jnp.asarray(depth_tables(nz)))
     sent = sent.reshape(devices, 4, 128)
     got = lax.all_to_all(sent, ROW_COL, 0, 0, tiled=True)
-    power, sums = plane_call(
-        got.reshape(devices * 4, 128), square, twiddle, shell.reshape(ny, nx), scale, unit
-    )
+    got = got.reshape(devices * 4, 128)
+    power, sums = plane_call(got, square, twiddle, shell.reshape(ny, nx), scale, unit)
     sums = sums + lax.ppermute(sums, CORE, [(0, 1), (1, 0)])
     chips = devices // lax.axis_size(CORE)
     sums = jnp.broadcast_to(sums, (chips, 2, 128))

time: 63.1 us -> 62.1 us (0.984)
  local copies, waits for them, and re-layouts: 2.13 us -> 0.06 us
  Pallas kernels: 3.97 us -> 5.08 us
    unnamed x10 -> x6, local copies, waits for them, and re-layouts: 2.09 us -> 0.02 us
    pallas_call x1, Pallas kernels: 0.52 us -> 1.69 us  [depth_call(): pl.pallas_call(depth_kernel, in_specs=[pl.BlockSpec(memory_space=pltpu.HB...]
where the time goes in v5:
time: 62.1 us; the launch traced here: 61.9 us
  blocking collectives  53.9 us (87%)
  Pallas kernels  5.08 us (8%)
  waiting for transfers between devices  0.82 us (1%)
  other arithmetic  0.71 us (1%)
  between operations  0.68 us (1%)
  starting transfers between devices  0.64 us (1%)
    all_to_all x1, blocking collectives, local(): got = lax.all_to_all(sent, ROW_COL, 0, 0, tiled=True)  36.6 us
    all_to_all x1, blocking collectives, local(): sums = lax.all_to_all(sums, CHIPS, 0, 0, tiled=True)  17.3 us
    pallas_call x1, Pallas kernels, plane_call(): pl.pallas_call(functools.partial(plane_kernel, scale, unit), out_shape=(j...  3.39 us
    pallas_call x1, Pallas kernels, depth_call(): pl.pallas_call(depth_kernel, in_specs=[pl.BlockSpec(memory_space=pltpu.HB...  1.69 us
  transfers between devices with their start and end apart: 1, of which 1 were waited for; matrix products, arithmetic and copies ran while one was open for 0% of the time, Pallas kernels for 0%

profile of v5, /device:TPU:1, one launch (start us, length us, event | category | flops | bytes accessed | tf_op | source)
XLA Modules:
  0.0 61.9 jit_solution(6590462176267988327)
XLA Ops:
  0.6 0.0 copy-start.2
  0.6 1.7 %depth.1 = f32[1024,128]{1,0:T(8,128)S(1)} custom-call(f32[256,512]{1,0:T(8,128)} %bitcast.9, bf16[2,2,256,256]{3,2,1,0:T(8,128)(2,1)} %constant.8.clone.table_hbm), custom_call_target="tpu_custom_call" | custom-call | tf_op jit(solution)/shard_map/depth/pallas_call | solution.py:175
  2.3 0.0 copy-start
  2.4 0.0 copy-start.1
  2.4 36.6 %all_to_all.10 = f32[256,4,128]{2,1,0:T(4,128)S(1)} all-to-all(f32[256,4,128]{2,1,0:T(4,128)S(1)} %bitcast.7), channel_id=1, replica_groups=mesh['row_0'=4,'row_1'=2,'row_2'=2,'col_0'=2,'col_1'=8] {'row_0','row_1'..., dimensions={0} | all-to-all | bytes 1048576 | tf_op jit(solution)/shard_map/all_to_all | solution.py:215
  39.0 0.0 copy-done.2
  39.0 0.0 copy-done
  39.0 0.0 copy-done.1
  39.0 3.4 %plane.1 = (f32[256,256]{1,0:T(8,128)}, f32[2,128]{1,0:T(2,128)S(1)}) custom-call(f32[1024,128]{1,0:T(8,128)S(1)} %bitcast.6, bf16[2,2,256,256]{3,2,1,0:T(8,128)(2,1)S(1)} %copy-done.1, f32[2,256,256]{2,1,0:T(8,128)S(1)} %copy-done, s32[256,256]{1,0:T(8,128)S(1)} %bitcast.8), custom_call_target="tpu_custom_call" | custom-call | tf_op jit(solution)/shard_map/plane/pallas_call | solution.py:191
  42.4 0.6 %collective-permute-start = (f32[2,128]{1,0:T(2,128)S(1)}, f32[2,128]{1,0:T(2,128)S(1)}, u32[]{:S(2)}, u32[]{:S(2)}) collective-permute-start(f32[2,128]{1,0:T(2,128)S(1)} %get-tuple-element.5), channel_id=1, source_target_pairs={{0,16},{16,0},{1,17},{17,1},{2,18},{18,2},{3,19},{19,3},{4,20},{20... | collective-permute-start | bytes 3080 | tf_op jit(solution)/shard_map/ppermute | solution.py:218
  43.1 0.8 %collective-permute-done = f32[2,128]{1,0:T(2,128)S(1)} collective-permute-done((f32[2,128]{1,0:T(2,128)S(1)}, f32[2,128]{1,0:T(2,128)S(1)}, u32[]{:S(2)}, u32[]{:S(2)}) %collective-permute-start) | collective-permute-done | bytes 1056 | tf_op jit(solution)/shard_map/ppermute | solution.py:218
  43.9 17.3 %all_to_all.11 = f32[128,2,128]{2,1,0:T(2,128)S(1)} all-to-all(f32[128,2,128]{2,1,0:T(2,128)S(1)} %broadcast_in_dim.3), channel_id=1, replica_groups=mesh['row_0'=4,'row_1'=2,'row_2'=2,'col_0'=2,'col_1'=8] {'row_0','row_1'..., dimensions={0} | all-to-all | bytes 262144 | tf_op jit(solution)/shard_map/all_to_all | solution.py:221
  61.2 0.7 %reduce_sum.9 = f32[2,128]{1,0:T(2,128)} reduce(f32[128,2,128]{2,1,0:T(2,128)S(1)} %all_to_all.11, f32[]{:T(128)} %constant.3.clone.1), dimensions={0}, to_apply=%region_0.0 | reduce | flops 32512 | bytes 132100 | tf_op jit(solution)/shard_map/reduce_sum | solution.py:222
  (2 shorter events, 0.0 us)
Async XLA Ops:
  0.6 38.4 %copy-start.2 = (s32[1,256,256]{2,1,0:T(8,128)S(1)}, s32[1,256,256]{2,1,0:T(8,128)}, u32[]{:S(2)}) copy-start(s32[1,256,256]{2,1,0:T(8,128)} %param.6) | copy-start | bytes 786436
  2.3 36.7 %copy-start = (f32[2,256,256]{2,1,0:T(8,128)S(1)}, f32[2,256,256]{2,1,0:T(8,128)}, u32[]{:S(2)}) copy-start(f32[2,256,256]{2,1,0:T(8,128)} %constant.10.clone.twiddle_ref) | copy-start | bytes 1572868
  2.4 36.7 %copy-start.1 = (bf16[2,2,256,256]{3,2,1,0:T(8,128)(2,1)S(1)}, bf16[2,2,256,256]{3,2,1,0:T(8,128)(2,1)}, u32[]{:S(2)}) copy-start(bf16[2,2,256,256]{3,2,1,0:T(8,128)(2,1)} %constant.9.clone.square_ref) | copy-start | bytes 1572868
  42.4 1.5 %collective-permute-start = (f32[2,128]{1,0:T(2,128)S(1)}, f32[2,128]{1,0:T(2,128)S(1)}, u32[]{:S(2)}, u32[]{:S(2)}) collective-permute-start(f32[2,128]{1,0:T(2,128)S(1)} %get-tuple-element.5), channel_id=1, source_target_pairs={{0,16},{16,0},{1,17},{17,1},{2,18},{18,2},{3,19},{19,3},{4,20},{20... | collective-permute-start | bytes 3080 | tf_op jit(solution)/shard_map/ppermute | solution.py:218

commit v6 on v5

--- a/solution.py
+++ b/solution.py
@@ -1,4 +1,5 @@
 import functools
+import itertools
 import math
 
 import jax
@@ -15,7 +16,8 @@
 COL = ("col_0", "col_1")
 ROW_COL = ROW + COL
 CORE = "row_2"
-CHIPS = ("row_0", "row_1", "col_0", "col_1")
+PEERS = ("row_0", "col_0", "col_1", "row_1", "row_2")
+CHIPS = ("col_1", "col_0", "row_0", "row_1")
 F32 = jnp.float32
 BF16 = jnp.bfloat16
 
@@ -26,30 +28,38 @@
     return np.stack([upper, lower])
 
 
+def peer_order(sizes):
+    ranks = np.arange(math.prod(sizes)).reshape(sizes)
+    return ranks.transpose([ROW_COL.index(axis) for axis in PEERS]).reshape(-1)
+
+
+def odd_step(sizes):
+    return math.prod(sizes[ROW_COL.index(axis)] for axis in PEERS[PEERS.index(COL[-1]) + 1 :])
+
+
 @functools.cache
-def depth_tables(nz):
-    half = nz // 2
-    freqs = nz // 4
-    z = np.arange(half)
+def depth_tables(nz, sizes):
+    order = peer_order(sizes).reshape(-1, 2, odd_step(sizes))
+    z = np.arange(nz // 2)
     out = []
     for parity in range(2):
-        k = 2 * np.arange(freqs) + parity
+        k = order[:, parity, :].T.reshape(-1)
         angle = 2.0 * math.pi / nz * (k[:, None] * z[None, :] % nz)
         out.append(split_table(np.concatenate([np.cos(angle), -np.sin(angle)])))
     return np.stack(out)
 
 
 @functools.cache
-def plane_tables(radix):
+def plane_tables(radix, sizes):
     n = np.arange(radix)
     base = np.multiply.outer(n, n)
     both = base[:, None, :, None] + base[None, :, None, :]
     both = both.reshape(radix * radix, radix * radix)
     angle = 2.0 * math.pi / radix * (both % radix)
     square = np.stack([split_table(np.cos(angle)), split_table(-np.sin(angle))])
-    angle = 2.0 * math.pi / (radix * radix) * (both % (radix * radix))
+    angle = 2.0 * math.pi / (radix * radix) * both
     twiddle = np.stack([np.cos(angle), -np.sin(angle)]).astype(np.float32)
-    return square, twiddle
+    return np.ascontiguousarray(square[..., peer_order(sizes)]), square, twiddle
 
 
 def split_two(values):
@@ -66,7 +76,7 @@
     return dot(lhs[0], rhs[0]) + dot(lhs[0], rhs[1]) + dot(lhs[1], rhs[0])
 
 
-def depth_kernel(field_hbm, table_hbm, out_ref, field_ref, table_ref, sems):
+def depth_kernel(step, field_hbm, table_hbm, out_ref, field_ref, table_ref, sems):
     copies = [
         pltpu.make_async_copy(field_hbm, field_ref, sems.at[0]),
         pltpu.make_async_copy(table_hbm, table_ref, sems.at[1]),
@@ -83,10 +93,12 @@
     for parity in range(2):
         folded = split_two(near + far if parity == 0 else near - far)
         spec = dot3((table_ref[parity, 0], table_ref[parity, 1]), folded, NT)
-        for part in range(2):
-            for side in range(2):
-                block = spec[part * freqs : (part + 1) * freqs, side * lanes : (side + 1) * lanes]
-                out_ref[pl.ds(parity * 4 + part * 2 + side, freqs, stride=8), :] = block
+        count = freqs // step
+        for part, low, side in itertools.product(range(2), range(step), range(2)):
+            start = part * freqs + low * count
+            block = spec[start : start + count, side * lanes : (side + 1) * lanes]
+            start = (parity * step + low) * 4 + part * 2 + side
+            out_ref[pl.ds(start, count, stride=8 * step), :] = block
 
 
 def swap_digits(blocks, radix):
@@ -108,7 +120,7 @@
 
 
 def plane_kernel(
-    scale, unit, recv_ref, square_ref, twiddle_ref, shell_ref, power_hbm, sums_ref, power_ref, sem
+    scale, unit, recv_ref, left_ref, right_ref, twiddle_ref, shell_ref, power_hbm, sums_ref, power_ref, sem
 ):
     n = power_ref.shape[0]
     radix = math.isqrt(n)
@@ -117,13 +129,15 @@
         for c in range(2)
     ]
     re, im = split_two(parts[0]), split_two(parts[1])
-    cos = (square_ref[0, 0], square_ref[0, 1])
-    sin = (square_ref[1, 0], square_ref[1, 1])
+    cos = (left_ref[0, 0], left_ref[0, 1])
+    sin = (left_ref[1, 0], left_ref[1, 1])
     u_re = dot3(cos, re, NN) - dot3(sin, im, NN)
     u_im = dot3(sin, re, NN) + dot3(cos, im, NN)
     t_re, t_im = twiddle_ref[0], twiddle_ref[1]
     re = split_two(u_re * t_re - u_im * t_im)
     im = split_two(u_re * t_im + u_im * t_re)
+    cos = (right_ref[0, 0], right_ref[0, 1])
+    sin = (right_ref[1, 0], right_ref[1, 1])
     v_re = dot3(re, cos, NN) - dot3(im, sin, NN)
     v_im = dot3(re, sin, NN) + dot3(im, cos, NN)
     power = (v_re * v_re + v_im * v_im) * scale
@@ -168,12 +182,12 @@
     copy.wait()
 
 
-def depth_call(field, tables):
+def depth_call(field, tables, step):
     rows = field.shape[0]
     field = pltpu.with_memory_space_constraint(field, pltpu.HBM)
     tables = pltpu.with_memory_space_constraint(tables, pltpu.HBM)
     return pl.pallas_call(
-        depth_kernel,
+        functools.partial(depth_kernel, step),
         in_specs=[pl.BlockSpec(memory_space=pltpu.HBM)] * 2,
         out_shape=jax.ShapeDtypeStruct((field.shape[1] // 2 * 4, rows // 2), F32),
         scratch_shapes=[
@@ -186,7 +200,7 @@
     )(field, tables)
 
 
-def plane_call(recv, square, twiddle, shell, scale, unit):
+def plane_call(recv, left, right, twiddle, shell, scale, unit):
     n = shell.shape[0]
     return pl.pallas_call(
         functools.partial(plane_kernel, scale, unit),
@@ -198,7 +212,7 @@
         scratch_shapes=[pltpu.VMEM((n, n), F32), pltpu.SemaphoreType.DMA],
         compiler_params=pltpu.CompilerParams(vmem_limit_bytes=24 << 20),
         name="plane",
-    )(recv, square, twiddle, shell)
+    )(recv, left, right, twiddle, shell)
 
 
 def local(field, shell):
@@ -207,14 +221,15 @@
     n_col = lax.axis_size(COL)
     devices = n_row * n_col
     nx, ny, keep = cx * n_row, cy * n_col, nz // 2
-    square, twiddle = plane_tables(n_row)
+    sizes = tuple(lax.axis_size(axis) for axis in ROW_COL)
+    left, right, twiddle = plane_tables(n_row, sizes)
     scale = 1.0 / (float(nx) * ny * nz)
     unit = float(SHELLS) / (keep * ny * nx)
-    sent = depth_call(field.reshape(cx * cy, nz), jnp.asarray(depth_tables(nz)))
+    sent = depth_call(field.reshape(cx * cy, nz), jnp.asarray(depth_tables(nz, sizes)), odd_step(sizes))
     sent = sent.reshape(devices, 4, 128)
-    got = lax.all_to_all(sent, ROW_COL, 0, 0, tiled=True)
+    got = lax.all_to_all(sent, PEERS, 0, 0, tiled=True)
     got = got.reshape(devices * 4, 128)
-    power, sums = plane_call(got, square, twiddle, shell.reshape(ny, nx), scale, unit)
+    power, sums = plane_call(got, left, right, twiddle, shell.reshape(ny, nx), scale, unit)
     sums = sums + lax.ppermute(sums, CORE, [(0, 1), (1, 0)])
     chips = devices // lax.axis_size(CORE)
     sums = jnp.broadcast_to(sums, (chips, 2, 128))

time: 62.1 us -> 61.3 us (0.987)
  blocking collectives: 53.9 us -> 53.1 us
    all_to_all x1, blocking collectives: 17.3 us -> 16.5 us  [local(): sums = lax.all_to_all(sums, CHIPS, 0, 0, tiled=True)]
where the time goes in v6:
time: 61.3 us; the launch traced here: 61.1 us
  blocking collectives  53.1 us (87%)
  Pallas kernels  5.34 us (9%)
  waiting for transfers between devices  1.15 us (2%)
  other arithmetic  0.71 us (1%)
  between operations  0.7 us (1%)
    all_to_all x1, blocking collectives, local(): got = lax.all_to_all(sent, PEERS, 0, 0, tiled=True)  36.6 us
    all_to_all x1, blocking collectives, local(): sums = lax.all_to_all(sums, CHIPS, 0, 0, tiled=True)  16.5 us
    pallas_call x1, Pallas kernels, plane_call(): pl.pallas_call(functools.partial(plane_kernel, scale, unit), out_shape=(j...  3.4 us
    pallas_call x1, Pallas kernels, depth_call(): pl.pallas_call(functools.partial(depth_kernel, step), in_specs=[pl.BlockS...  1.94 us
  transfers between devices with their start and end apart: 1, of which 1 were waited for; matrix products, arithmetic and copies ran while one was open for 0% of the time, Pallas kernels for 0%

profile of v6, /device:TPU:1, one launch (start us, length us, event | category | flops | bytes accessed | tf_op | source)
XLA Modules:
  0.0 61.1 jit_solution(2077454763213788539)
XLA Ops:
  0.6 0.0 copy-start.2
  0.6 0.0 copy-start.3
  0.7 1.9 %depth.1 = f32[1024,128]{1,0:T(8,128)S(1)} custom-call(f32[256,512]{1,0:T(8,128)} %bitcast.9, bf16[2,2,256,256]{3,2,1,0:T(8,128)(2,1)} %constant.10.clone.table_hbm), custom_call_target="tpu_custom_call" | custom-call | tf_op jit(solution)/shard_map/depth/pallas_call | solution.py:189
  2.6 0.0 copy-start
  2.6 0.0 copy-start.1
  2.6 36.6 %all_to_all.10 = f32[256,4,128]{2,1,0:T(4,128)S(1)} all-to-all(f32[256,4,128]{2,1,0:T(4,128)S(1)} %bitcast.6), channel_id=1, replica_groups=mesh['row_0'=4,'row_1'=2,'row_2'=2,'col_0'=2,'col_1'=8] {'row_0','col_0'..., dimensions={0} | all-to-all | bytes 1048576 | tf_op jit(solution)/shard_map/all_to_all | solution.py:230
  39.2 0.0 copy-done.2
  39.2 0.0 copy-done.3
  39.2 0.0 copy-done
  39.2 0.0 copy-done.1
  39.3 3.4 %plane.1 = (f32[256,256]{1,0:T(8,128)}, f32[2,128]{1,0:T(2,128)S(1)}) custom-call(f32[1024,128]{1,0:T(8,128)S(1)} %bitcast.7, bf16[2,2,256,256]{3,2,1,0:T(8,128)(2,1)S(1)} %copy-done.2, bf16[2,2,256,256]{3,2,1,0:T(8,128)(2,1)S(1)} %copy-done.1, f32[2,256,256]{2,1,0:T(8,128)S(1)} %copy-done, s32[256,256]{1,0:T(8,128)S(1)} %bitcast.8), custom_call_target="tpu_custom_call" | custom-call | tf_op jit(solution)/shard_map/plane/pallas_call | solution.py:205
  42.7 0.1 collective-permute-start
  42.8 1.1 %collective-permute-done = f32[2,128]{1,0:T(2,128)S(1)} collective-permute-done((f32[2,128]{1,0:T(2,128)S(1)}, f32[2,128]{1,0:T(2,128)S(1)}, u32[]{:S(2)}, u32[]{:S(2)}) %collective-permute-start) | collective-permute-done | bytes 1056 | tf_op jit(solution)/shard_map/ppermute | solution.py:233
  44.0 16.5 %all_to_all.11 = f32[128,2,128]{2,1,0:T(2,128)S(1)} all-to-all(f32[128,2,128]{2,1,0:T(2,128)S(1)} %broadcast_in_dim.3), channel_id=1, replica_groups=mesh['row_0'=4,'row_1'=2,'row_2'=2,'col_0'=2,'col_1'=8] {'col_1','col_0'..., dimensions={0} | all-to-all | bytes 262144 | tf_op jit(solution)/shard_map/all_to_all | solution.py:236
  60.4 0.7 %reduce_sum.9 = f32[2,128]{1,0:T(2,128)} reduce(f32[128,2,128]{2,1,0:T(2,128)S(1)} %all_to_all.11, f32[]{:T(128)} %constant.4.clone.1), dimensions={0}, to_apply=%region_0.0 | reduce | flops 32512 | bytes 132100 | tf_op jit(solution)/shard_map/reduce_sum | solution.py:237
  (2 shorter events, 0.0 us)
Async XLA Ops:
  0.6 38.6 %copy-start.2 = (bf16[2,2,256,256]{3,2,1,0:T(8,128)(2,1)S(1)}, bf16[2,2,256,256]{3,2,1,0:T(8,128)(2,1)}, u32[]{:S(2)}) copy-start(bf16[2,2,256,256]{3,2,1,0:T(8,128)(2,1)} %constant.11.clone.left_ref) | copy-start | bytes 1572868
  0.6 38.6 %copy-start.3 = (s32[1,256,256]{2,1,0:T(8,128)S(1)}, s32[1,256,256]{2,1,0:T(8,128)}, u32[]{:S(2)}) copy-start(s32[1,256,256]{2,1,0:T(8,128)} %param.7) | copy-start | bytes 786436
  2.6 36.6 %copy-start = (f32[2,256,256]{2,1,0:T(8,128)S(1)}, f32[2,256,256]{2,1,0:T(8,128)}, u32[]{:S(2)}) copy-start(f32[2,256,256]{2,1,0:T(8,128)} %constant.13.clone.twiddle_ref) | copy-start | bytes 1572868
  2.6 36.6 %copy-start.1 = (bf16[2,2,256,256]{3,2,1,0:T(8,128)(2,1)S(1)}, bf16[2,2,256,256]{3,2,1,0:T(8,128)(2,1)}, u32[]{:S(2)}) copy-start(bf16[2,2,256,256]{3,2,1,0:T(8,128)(2,1)} %constant.12.clone.right_ref) | copy-start | bytes 1572868
  42.7 1.2 %collective-permute-start = (f32[2,128]{1,0:T(2,128)S(1)}, f32[2,128]{1,0:T(2,128)S(1)}, u32[]{:S(2)}, u32[]{:S(2)}) collective-permute-start(f32[2,128]{1,0:T(2,128)S(1)} %get-tuple-element.5), channel_id=1, source_target_pairs={{0,16},{16,0},{1,17},{17,1},{2,18},{18,2},{3,19},{19,3},{4,20},{20... | collective-permute-start | bytes 3080 | tf_op jit(solution)/shard_map/ppermute | solution.py:233

commit v7 on v6

--- a/solution.py
+++ b/solution.py
@@ -16,7 +16,7 @@
 COL = ("col_0", "col_1")
 ROW_COL = ROW + COL
 CORE = "row_2"
-PEERS = ("row_0", "col_0", "col_1", "row_1", "row_2")
+PEERS = ("col_0", "row_1", "row_0", "col_1", "row_2")
 CHIPS = ("col_1", "col_0", "row_0", "row_1")
 F32 = jnp.float32
 BF16 = jnp.bfloat16
@@ -77,20 +77,22 @@
 
 
 def depth_kernel(step, field_hbm, table_hbm, out_ref, field_ref, table_ref, sems):
-    copies = [
-        pltpu.make_async_copy(field_hbm, field_ref, sems.at[0]),
-        pltpu.make_async_copy(table_hbm, table_ref, sems.at[1]),
+    tables = [
+        pltpu.make_async_copy(table_hbm.at[parity], table_ref.at[parity], sems.at[parity])
+        for parity in range(2)
     ]
-    for copy in copies:
-        copy.start()
-    for copy in copies:
-        copy.wait()
+    whole = pltpu.make_async_copy(field_hbm, field_ref, sems.at[2])
+    tables[0].start()
+    whole.start()
+    tables[1].start()
+    whole.wait()
     half = field_ref.shape[1] // 2
     lanes = field_ref.shape[0] // 2
     freqs = table_ref.shape[2] // 2
     near = field_ref[:, :half]
     far = field_ref[:, half:]
     for parity in range(2):
+        tables[parity].wait()
         folded = split_two(near + far if parity == 0 else near - far)
         spec = dot3((table_ref[parity, 0], table_ref[parity, 1]), folded, NT)
         count = freqs // step
@@ -193,7 +195,7 @@
         scratch_shapes=[
             pltpu.VMEM(field.shape, field.dtype),
             pltpu.VMEM(tables.shape, tables.dtype),
-            pltpu.SemaphoreType.DMA((2,)),
+            pltpu.SemaphoreType.DMA((3,)),
         ],
         compiler_params=pltpu.CompilerParams(vmem_limit_bytes=12 << 20),
         name="depth",

time: 61.3 us -> 61.4 us (level)
  starting transfers between devices: 0.09 us -> 0.74 us
    all_to_all x1, blocking collectives: 36.6 us -> 35.6 us  [local(): got = lax.all_to_all(sent, PEERS, 0, 0, tiled=True)]
    ppermute x1, starting transfers between devices: 0.09 us -> 0.74 us  [local(): sums = sums + lax.ppermute(sums, CORE, [(0, 1), (1, 0)])]
    all_to_all x1, blocking collectives: 16.5 us -> 17.1 us  [local(): sums = lax.all_to_all(sums, CHIPS, 0, 0, tiled=True)]
where the time goes in v7:
time: 61.4 us; the launch traced here: 61.2 us
  blocking collectives  52.6 us (86%)
  Pallas kernels  5.51 us (9%)
  waiting for transfers between devices  0.82 us (1%)
  starting transfers between devices  0.74 us (1%)
  other arithmetic  0.71 us (1%)
  between operations  0.69 us (1%)
    all_to_all x1, blocking collectives, local(): got = lax.all_to_all(sent, PEERS, 0, 0, tiled=True)  35.6 us
    all_to_all x1, blocking collectives, local(): sums = lax.all_to_all(sums, CHIPS, 0, 0, tiled=True)  17.1 us
    pallas_call x1, Pallas kernels, plane_call(): pl.pallas_call(functools.partial(plane_kernel, scale, unit), out_shape=(j...  3.41 us
    pallas_call x1, Pallas kernels, depth_call(): pl.pallas_call(functools.partial(depth_kernel, step), in_specs=[pl.BlockS...  2.1 us
  transfers between devices with their start and end apart: 1, of which 1 were waited for; matrix products, arithmetic and copies ran while one was open for 0% of the time, Pallas kernels for 0%

profile of v7, /device:TPU:1, one launch (start us, length us, event | category | flops | bytes accessed | tf_op | source)
XLA Modules:
  0.0 61.2 jit_solution(8523562574138316053)
XLA Ops:
  0.6 0.0 copy-start.2
  0.6 0.0 copy-start.3
  0.7 2.1 %depth.1 = f32[1024,128]{1,0:T(8,128)S(1)} custom-call(f32[256,512]{1,0:T(8,128)} %bitcast.9, bf16[2,2,256,256]{3,2,1,0:T(8,128)(2,1)} %constant.10.clone.table_hbm), custom_call_target="tpu_custom_call" | custom-call | tf_op jit(solution)/shard_map/depth/pallas_call | solution.py:191
  2.8 0.0 copy-start
  2.8 0.0 copy-start.1
  2.8 35.6 %all_to_all.10 = f32[256,4,128]{2,1,0:T(4,128)S(1)} all-to-all(f32[256,4,128]{2,1,0:T(4,128)S(1)} %bitcast.6), channel_id=1, replica_groups=mesh['row_0'=4,'row_1'=2,'row_2'=2,'col_0'=2,'col_1'=8] {'col_0','row_1'..., dimensions={0} | all-to-all | bytes 1048576 | tf_op jit(solution)/shard_map/all_to_all | solution.py:232
  38.4 0.0 copy-done.2
  38.4 0.0 copy-done.3
  38.4 0.0 copy-done
  38.4 0.0 copy-done.1
  38.4 3.4 %plane.1 = (f32[256,256]{1,0:T(8,128)}, f32[2,128]{1,0:T(2,128)S(1)}) custom-call(f32[1024,128]{1,0:T(8,128)S(1)} %bitcast.7, bf16[2,2,256,256]{3,2,1,0:T(8,128)(2,1)S(1)} %copy-done.2, bf16[2,2,256,256]{3,2,1,0:T(8,128)(2,1)S(1)} %copy-done.1, f32[2,256,256]{2,1,0:T(8,128)S(1)} %copy-done, s32[256,256]{1,0:T(8,128)S(1)} %bitcast.8), custom_call_target="tpu_custom_call" | custom-call | tf_op jit(solution)/shard_map/plane/pallas_call | solution.py:207
  41.8 0.7 %collective-permute-start = (f32[2,128]{1,0:T(2,128)S(1)}, f32[2,128]{1,0:T(2,128)S(1)}, u32[]{:S(2)}, u32[]{:S(2)}) collective-permute-start(f32[2,128]{1,0:T(2,128)S(1)} %get-tuple-element.5), channel_id=1, source_target_pairs={{0,16},{16,0},{1,17},{17,1},{2,18},{18,2},{3,19},{19,3},{4,20},{20... | collective-permute-start | bytes 3080 | tf_op jit(solution)/shard_map/ppermute | solution.py:235
  42.5 0.8 %collective-permute-done = f32[2,128]{1,0:T(2,128)S(1)} collective-permute-done((f32[2,128]{1,0:T(2,128)S(1)}, f32[2,128]{1,0:T(2,128)S(1)}, u32[]{:S(2)}, u32[]{:S(2)}) %collective-permute-start) | collective-permute-done | bytes 1056 | tf_op jit(solution)/shard_map/ppermute | solution.py:235
  43.4 17.1 %all_to_all.11 = f32[128,2,128]{2,1,0:T(2,128)S(1)} all-to-all(f32[128,2,128]{2,1,0:T(2,128)S(1)} %broadcast_in_dim.3), channel_id=1, replica_groups=mesh['row_0'=4,'row_1'=2,'row_2'=2,'col_0'=2,'col_1'=8] {'col_1','col_0'..., dimensions={0} | all-to-all | bytes 262144 | tf_op jit(solution)/shard_map/all_to_all | solution.py:238
  60.5 0.7 %reduce_sum.9 = f32[2,128]{1,0:T(2,128)} reduce(f32[128,2,128]{2,1,0:T(2,128)S(1)} %all_to_all.11, f32[]{:T(128)} %constant.4.clone.1), dimensions={0}, to_apply=%region_0.0 | reduce | flops 32512 | bytes 132100 | tf_op jit(solution)/shard_map/reduce_sum | solution.py:239
  (2 shorter events, 0.0 us)
Async XLA Ops:
  0.6 37.7 %copy-start.2 = (bf16[2,2,256,256]{3,2,1,0:T(8,128)(2,1)S(1)}, bf16[2,2,256,256]{3,2,1,0:T(8,128)(2,1)}, u32[]{:S(2)}) copy-start(bf16[2,2,256,256]{3,2,1,0:T(8,128)(2,1)} %constant.11.clone.left_ref) | copy-start | bytes 1572868
  0.6 37.7 %copy-start.3 = (s32[1,256,256]{2,1,0:T(8,128)S(1)}, s32[1,256,256]{2,1,0:T(8,128)}, u32[]{:S(2)}) copy-start(s32[1,256,256]{2,1,0:T(8,128)} %param.7) | copy-start | bytes 786436
  2.8 35.6 %copy-start = (f32[2,256,256]{2,1,0:T(8,128)S(1)}, f32[2,256,256]{2,1,0:T(8,128)}, u32[]{:S(2)}) copy-start(f32[2,256,256]{2,1,0:T(8,128)} %constant.13.clone.twiddle_ref) | copy-start | bytes 1572868
  2.8 35.6 %copy-start.1 = (bf16[2,2,256,256]{3,2,1,0:T(8,128)(2,1)S(1)}, bf16[2,2,256,256]{3,2,1,0:T(8,128)(2,1)}, u32[]{:S(2)}) copy-start(bf16[2,2,256,256]{3,2,1,0:T(8,128)(2,1)} %constant.12.clone.right_ref) | copy-start | bytes 1572868
  41.8 1.6 %collective-permute-start = (f32[2,128]{1,0:T(2,128)S(1)}, f32[2,128]{1,0:T(2,128)S(1)}, u32[]{:S(2)}, u32[]{:S(2)}) collective-permute-start(f32[2,128]{1,0:T(2,128)S(1)} %get-tuple-element.5), channel_id=1, source_target_pairs={{0,16},{16,0},{1,17},{17,1},{2,18},{18,2},{3,19},{19,3},{4,20},{20... | collective-permute-start | bytes 3080 | tf_op jit(solution)/shard_map/ppermute | solution.py:235

commit v8 on v6

--- a/solution.py
+++ b/solution.py
@@ -120,8 +120,14 @@
 
 
 def plane_kernel(
-    scale, unit, recv_ref, left_ref, right_ref, twiddle_ref, shell_ref, power_hbm, sums_ref, power_ref, sem
+    scale, unit, recv_ref, left_ref, twiddle_ref, right_hbm, shell_hbm, power_hbm, sums_ref, power_ref, right_ref, shell_ref, sems
 ):
+    more = [
+        pltpu.make_async_copy(right_hbm, right_ref, sems.at[0]),
+        pltpu.make_async_copy(shell_hbm, shell_ref, sems.at[1]),
+    ]
+    for copy in more:
+        copy.start()
     n = power_ref.shape[0]
     radix = math.isqrt(n)
     parts = [
@@ -136,12 +142,14 @@
     t_re, t_im = twiddle_ref[0], twiddle_ref[1]
     re = split_two(u_re * t_re - u_im * t_im)
     im = split_two(u_re * t_im + u_im * t_re)
+    more[0].wait()
     cos = (right_ref[0, 0], right_ref[0, 1])
     sin = (right_ref[1, 0], right_ref[1, 1])
     v_re = dot3(re, cos, NN) - dot3(im, sin, NN)
     v_im = dot3(re, sin, NN) + dot3(im, cos, NN)
     power = (v_re * v_re + v_im * v_im) * scale
     half = n // 2
+    more[1].wait()
     picks = []
     marked = []
     for side in range(2):
@@ -162,7 +170,7 @@
             flags = [low == jnp.array(l, BF16) for l in range(16)]
             picked = [jnp.where(flag, one, zero) for flag in flags]
             marked.append(jnp.concatenate(picked, axis=0))
-    copy = pltpu.make_async_copy(power_ref, power_hbm, sem)
+    copy = pltpu.make_async_copy(power_ref, power_hbm, sems.at[2])
     copy.start()
     dot = functools.partial(lax.dot_general, preferred_element_type=F32)
     acc = dot(jnp.concatenate(picks, axis=1), jnp.concatenate(marked, axis=1), NT)
@@ -202,17 +210,25 @@
 
 def plane_call(recv, left, right, twiddle, shell, scale, unit):
     n = shell.shape[0]
+    right = pltpu.with_memory_space_constraint(jnp.asarray(right), pltpu.HBM)
+    shell = pltpu.with_memory_space_constraint(shell, pltpu.HBM)
     return pl.pallas_call(
         functools.partial(plane_kernel, scale, unit),
         out_shape=(
             jax.ShapeDtypeStruct((n, n), F32),
             jax.ShapeDtypeStruct((2, 128), F32),
         ),
+        in_specs=[pl.BlockSpec(memory_space=pltpu.VMEM)] * 3 + [pl.BlockSpec(memory_space=pltpu.HBM)] * 2,
         out_specs=(pl.BlockSpec(memory_space=pltpu.HBM), pl.BlockSpec(memory_space=pltpu.VMEM)),
-        scratch_shapes=[pltpu.VMEM((n, n), F32), pltpu.SemaphoreType.DMA],
+        scratch_shapes=[
+            pltpu.VMEM((n, n), F32),
+            pltpu.VMEM(right.shape, right.dtype),
+            pltpu.VMEM(shell.shape, shell.dtype),
+            pltpu.SemaphoreType.DMA((3,)),
+        ],
         compiler_params=pltpu.CompilerParams(vmem_limit_bytes=24 << 20),
         name="plane",
-    )(recv, left, right, twiddle, shell)
+    )(recv, left, twiddle, right, shell)
 
 
 def local(field, shell):

time: 61.3 us -> 61.5 us (level)
  no operation moved by 1% of the time
where the time goes in v8:
time: 61.5 us; the launch traced here: 61.3 us
  blocking collectives  53.1 us (86%)
  Pallas kernels  5.56 us (9%)
  waiting for transfers between devices  1.15 us (2%)
  other arithmetic  0.71 us (1%)
  between operations  0.68 us (1%)
    all_to_all x1, blocking collectives, local(): got = lax.all_to_all(sent, PEERS, 0, 0, tiled=True)  36.6 us
    all_to_all x1, blocking collectives, local(): sums = lax.all_to_all(sums, CHIPS, 0, 0, tiled=True)  16.5 us
    pallas_call x1, Pallas kernels, plane_call(): pl.pallas_call(functools.partial(plane_kernel, scale, unit), out_shape=(j...  3.7 us
    pallas_call x1, Pallas kernels, depth_call(): pl.pallas_call(functools.partial(depth_kernel, step), in_specs=[pl.BlockS...  1.87 us
  transfers between devices with their start and end apart: 1, of which 1 were waited for; matrix products, arithmetic and copies ran while one was open for 0% of the time, Pallas kernels for 0%

profile of v8, /device:TPU:1, one launch (start us, length us, event | category | flops | bytes accessed | tf_op | source)
XLA Modules:
  0.0 61.3 jit_solution(5733732421872313656)
XLA Ops:
  0.6 1.9 %depth.1 = f32[1024,128]{1,0:T(8,128)S(1)} custom-call(f32[256,512]{1,0:T(8,128)} %bitcast.8, bf16[2,2,256,256]{3,2,1,0:T(8,128)(2,1)} %constant.10.clone.table_hbm), custom_call_target="tpu_custom_call" | custom-call | tf_op jit(solution)/shard_map/depth/pallas_call | solution.py:197
  2.5 0.0 copy-start
  2.5 0.0 copy-start.1
  2.5 36.6 %all_to_all.10 = f32[256,4,128]{2,1,0:T(4,128)S(1)} all-to-all(f32[256,4,128]{2,1,0:T(4,128)S(1)} %bitcast.6), channel_id=1, replica_groups=mesh['row_0'=4,'row_1'=2,'row_2'=2,'col_0'=2,'col_1'=8] {'row_0','col_0'..., dimensions={0} | all-to-all | bytes 1048576 | tf_op jit(solution)/shard_map/all_to_all | solution.py:246
  39.1 0.0 copy-done
  39.1 0.0 copy-done.1
  39.1 3.7 %plane.1 = (f32[256,256]{1,0:T(8,128)}, f32[2,128]{1,0:T(2,128)S(1)}) custom-call(f32[1024,128]{1,0:T(8,128)S(1)} %bitcast.7, bf16[2,2,256,256]{3,2,1,0:T(8,128)(2,1)S(1)} %copy-done.1, f32[2,256,256]{2,1,0:T(8,128)S(1)} %copy-done, bf16[2,2,256,256]{3,2,1,0:T(8,128)(2,1)} %constant.11.clone.right_hbm, s32[256,256]{1,0:T(8,128)} %bitcast.9), custom_call_target="tpu_custom_call" | custom-call | tf_op jit(solution)/shard_map/plane/pallas_call | solution.py:215
  42.8 0.1 collective-permute-start
  42.9 1.1 %collective-permute-done = f32[2,128]{1,0:T(2,128)S(1)} collective-permute-done((f32[2,128]{1,0:T(2,128)S(1)}, f32[2,128]{1,0:T(2,128)S(1)}, u32[]{:S(2)}, u32[]{:S(2)}) %collective-permute-start) | collective-permute-done | bytes 1056 | tf_op jit(solution)/shard_map/ppermute | solution.py:249
  44.1 16.5 %all_to_all.11 = f32[128,2,128]{2,1,0:T(2,128)S(1)} all-to-all(f32[128,2,128]{2,1,0:T(2,128)S(1)} %broadcast_in_dim.3), channel_id=1, replica_groups=mesh['row_0'=4,'row_1'=2,'row_2'=2,'col_0'=2,'col_1'=8] {'col_1','col_0'..., dimensions={0} | all-to-all | bytes 262144 | tf_op jit(solution)/shard_map/all_to_all | solution.py:252
  60.6 0.7 %reduce_sum.9 = f32[2,128]{1,0:T(2,128)} reduce(f32[128,2,128]{2,1,0:T(2,128)S(1)} %all_to_all.11, f32[]{:T(128)} %constant.4.clone.1), dimensions={0}, to_apply=%region_0.0 | reduce | flops 32512 | bytes 132100 | tf_op jit(solution)/shard_map/reduce_sum | solution.py:253
  (2 shorter events, 0.0 us)
Async XLA Ops:
  2.5 36.6 %copy-start = (f32[2,256,256]{2,1,0:T(8,128)S(1)}, f32[2,256,256]{2,1,0:T(8,128)}, u32[]{:S(2)}) copy-start(f32[2,256,256]{2,1,0:T(8,128)} %constant.13.clone.twiddle_ref) | copy-start | bytes 1572868
  2.5 36.6 %copy-start.1 = (bf16[2,2,256,256]{3,2,1,0:T(8,128)(2,1)S(1)}, bf16[2,2,256,256]{3,2,1,0:T(8,128)(2,1)}, u32[]{:S(2)}) copy-start(bf16[2,2,256,256]{3,2,1,0:T(8,128)(2,1)} %constant.12.clone.left_ref) | copy-start | bytes 1572868
  42.8 1.2 %collective-permute-start = (f32[2,128]{1,0:T(2,128)S(1)}, f32[2,128]{1,0:T(2,128)S(1)}, u32[]{:S(2)}, u32[]{:S(2)}) collective-permute-start(f32[2,128]{1,0:T(2,128)S(1)} %get-tuple-element.5), channel_id=1, source_target_pairs={{0,16},{16,0},{1,17},{17,1},{2,18},{18,2},{3,19},{19,3},{4,20},{20... | collective-permute-start | bytes 3080 | tf_op jit(solution)/shard_map/ppermute | solution.py:249

commit v9 on v6

--- a/solution.py
+++ b/solution.py
@@ -13,11 +13,11 @@
 
 SHELLS = 256
 ROW = ("row_0", "row_1", "row_2")
-COL = ("col_0", "col_1")
+COL = ("col_0", "col_1", "col_2")
 ROW_COL = ROW + COL
 CORE = "row_2"
-PEERS = ("row_0", "col_0", "col_1", "row_1", "row_2")
-CHIPS = ("col_1", "col_0", "row_0", "row_1")
+PEERS = ("row_0", "col_0", "col_1", "row_1", "row_2", "col_2")
+CHIPS = ("col_1", "col_2", "col_0", "row_0", "row_1")
 F32 = jnp.float32
 BF16 = jnp.bfloat16
 
@@ -239,7 +239,7 @@
 
 
 def solution(mesh):
-    split = Mesh(mesh.devices.reshape(4, 2, 2, 2, 8), ROW_COL)
+    split = Mesh(mesh.devices.reshape(4, 2, 2, 2, 4, 2), ROW_COL)
     in_specs = (P(None, ROW, COL, None), P(ROW_COL, None, None))
     out_specs = (P(None, ROW_COL, None, None), P())
     return jax.shard_map(local, mesh=split, in_specs=in_specs, out_specs=out_specs, check_vma=False)

time: 61.3 us -> 61.3 us (level)
  starting transfers between devices: 0.09 us -> 1.61 us
  blocking collectives: 53.1 us -> 52.2 us
    ppermute x1, starting transfers between devices: 0.09 us -> 1.61 us  [local(): sums = sums + lax.ppermute(sums, CORE, [(0, 1), (1, 0)])]
    all_to_all x1, blocking collectives: 36.6 us -> 35.8 us  [local(): got = lax.all_to_all(sent, PEERS, 0, 0, tiled=True)]
where the time goes in v9:
time: 61.3 us; the launch traced here: 61.2 us
  blocking collectives  52.2 us (85%)
  Pallas kernels  5.12 us (8%)
  starting transfers between devices  1.61 us (3%)
  waiting for transfers between devices  0.82 us (1%)
  other arithmetic  0.71 us (1%)
  between operations  0.69 us (1%)
    all_to_all x1, blocking collectives, local(): got = lax.all_to_all(sent, PEERS, 0, 0, tiled=True)  35.8 us
    all_to_all x1, blocking collectives, local(): sums = lax.all_to_all(sums, CHIPS, 0, 0, tiled=True)  16.3 us
    pallas_call x1, Pallas kernels, plane_call(): pl.pallas_call(functools.partial(plane_kernel, scale, unit), out_shape=(j...  3.4 us
    pallas_call x1, Pallas kernels, depth_call(): pl.pallas_call(functools.partial(depth_kernel, step), in_specs=[pl.BlockS...  1.72 us
    ppermute x1, starting transfers between devices, local(): sums = sums + lax.ppermute(sums, CORE, [(0, 1), (1, 0)])  1.61 us
  transfers between devices with their start and end apart: 1, of which 1 were waited for; matrix products, arithmetic and copies ran while one was open for 0% of the time, Pallas kernels for 0%

profile of v9, /device:TPU:1, one launch (start us, length us, event | category | flops | bytes accessed | tf_op | source)
XLA Modules:
  0.0 61.2 jit_solution(6602108346179710291)
XLA Ops:
  0.6 0.0 copy-start.2
  0.6 0.0 copy-start.3
  0.7 1.7 %depth.1 = f32[1024,128]{1,0:T(8,128)S(1)} custom-call(f32[256,512]{1,0:T(8,128)} %bitcast.9, bf16[2,2,256,256]{3,2,1,0:T(8,128)(2,1)} %constant.10.clone.table_hbm), custom_call_target="tpu_custom_call" | custom-call | tf_op jit(solution)/shard_map/depth/pallas_call | solution.py:189
  2.4 0.0 copy-start
  2.4 0.0 copy-start.1
  2.4 35.8 %all_to_all.10 = f32[256,4,128]{2,1,0:T(4,128)S(1)} all-to-all(f32[256,4,128]{2,1,0:T(4,128)S(1)} %bitcast.6), channel_id=1, replica_groups=mesh['row_0'=4,'row_1'=2,'row_2'=2,'col_0'=2,'col_1'=4,'col_2'=2] {'row_..., dimensions={0} | all-to-all | bytes 1048576 | tf_op jit(solution)/shard_map/all_to_all | solution.py:230
  38.2 0.0 copy-done.2
  38.2 0.0 copy-done.3
  38.2 0.0 copy-done
  38.2 0.0 copy-done.1
  38.2 3.4 %plane.1 = (f32[256,256]{1,0:T(8,128)}, f32[2,128]{1,0:T(2,128)S(1)}) custom-call(f32[1024,128]{1,0:T(8,128)S(1)} %bitcast.7, bf16[2,2,256,256]{3,2,1,0:T(8,128)(2,1)S(1)} %copy-done.2, bf16[2,2,256,256]{3,2,1,0:T(8,128)(2,1)S(1)} %copy-done.1, f32[2,256,256]{2,1,0:T(8,128)S(1)} %copy-done, s32[256,256]{1,0:T(8,128)S(1)} %bitcast.8), custom_call_target="tpu_custom_call" | custom-call | tf_op jit(solution)/shard_map/plane/pallas_call | solution.py:205
  41.6 1.6 %collective-permute-start = (f32[2,128]{1,0:T(2,128)S(1)}, f32[2,128]{1,0:T(2,128)S(1)}, u32[]{:S(2)}, u32[]{:S(2)}) collective-permute-start(f32[2,128]{1,0:T(2,128)S(1)} %get-tuple-element.5), channel_id=1, source_target_pairs={{0,16},{16,0},{1,17},{17,1},{2,18},{18,2},{3,19},{19,3},{4,20},{20... | collective-permute-start | bytes 3080 | tf_op jit(solution)/shard_map/ppermute | solution.py:233
  43.3 0.8 %collective-permute-done = f32[2,128]{1,0:T(2,128)S(1)} collective-permute-done((f32[2,128]{1,0:T(2,128)S(1)}, f32[2,128]{1,0:T(2,128)S(1)}, u32[]{:S(2)}, u32[]{:S(2)}) %collective-permute-start) | collective-permute-done | bytes 1056 | tf_op jit(solution)/shard_map/ppermute | solution.py:233
  44.1 16.3 %all_to_all.11 = f32[128,2,128]{2,1,0:T(2,128)S(1)} all-to-all(f32[128,2,128]{2,1,0:T(2,128)S(1)} %broadcast_in_dim.3), channel_id=1, replica_groups=mesh['row_0'=4,'row_1'=2,'row_2'=2,'col_0'=2,'col_1'=4,'col_2'=2] {'col_..., dimensions={0} | all-to-all | bytes 262144 | tf_op jit(solution)/shard_map/all_to_all | solution.py:236
  60.5 0.7 %reduce_sum.9 = f32[2,128]{1,0:T(2,128)} reduce(f32[128,2,128]{2,1,0:T(2,128)S(1)} %all_to_all.11, f32[]{:T(128)} %constant.4.clone.1), dimensions={0}, to_apply=%region_0.0 | reduce | flops 32512 | bytes 132100 | tf_op jit(solution)/shard_map/reduce_sum | solution.py:237
  (2 shorter events, 0.0 us)
Async XLA Ops:
  0.6 37.6 %copy-start.2 = (bf16[2,2,256,256]{3,2,1,0:T(8,128)(2,1)S(1)}, bf16[2,2,256,256]{3,2,1,0:T(8,128)(2,1)}, u32[]{:S(2)}) copy-start(bf16[2,2,256,256]{3,2,1,0:T(8,128)(2,1)} %constant.11.clone.left_ref) | copy-start | bytes 1572868
  0.6 37.6 %copy-start.3 = (s32[1,256,256]{2,1,0:T(8,128)S(1)}, s32[1,256,256]{2,1,0:T(8,128)}, u32[]{:S(2)}) copy-start(s32[1,256,256]{2,1,0:T(8,128)} %param.7) | copy-start | bytes 786436
  2.4 35.8 %copy-start = (f32[2,256,256]{2,1,0:T(8,128)S(1)}, f32[2,256,256]{2,1,0:T(8,128)}, u32[]{:S(2)}) copy-start(f32[2,256,256]{2,1,0:T(8,128)} %constant.13.clone.twiddle_ref) | copy-start | bytes 1572868
  2.4 35.8 %copy-start.1 = (bf16[2,2,256,256]{3,2,1,0:T(8,128)(2,1)S(1)}, bf16[2,2,256,256]{3,2,1,0:T(8,128)(2,1)}, u32[]{:S(2)}) copy-start(bf16[2,2,256,256]{3,2,1,0:T(8,128)(2,1)} %constant.12.clone.right_ref) | copy-start | bytes 1572868
  41.6 2.4 %collective-permute-start = (f32[2,128]{1,0:T(2,128)S(1)}, f32[2,128]{1,0:T(2,128)S(1)}, u32[]{:S(2)}, u32[]{:S(2)}) collective-permute-start(f32[2,128]{1,0:T(2,128)S(1)} %get-tuple-element.5), channel_id=1, source_target_pairs={{0,16},{16,0},{1,17},{17,1},{2,18},{18,2},{3,19},{19,3},{4,20},{20... | collective-permute-start | bytes 3080 | tf_op jit(solution)/shard_map/ppermute | solution.py:233

commit v10 on v9

--- a/solution.py
+++ b/solution.py
@@ -56,7 +56,8 @@
     both = base[:, None, :, None] + base[None, :, None, :]
     both = both.reshape(radix * radix, radix * radix)
     angle = 2.0 * math.pi / radix * (both % radix)
-    square = np.stack([split_table(np.cos(angle)), split_table(-np.sin(angle))])
+    cos, sin = np.cos(angle), -np.sin(angle)
+    square = np.stack([split_table(table) for table in (cos, sin - cos, cos + sin)])
     angle = 2.0 * math.pi / (radix * radix) * both
     twiddle = np.stack([np.cos(angle), -np.sin(angle)]).astype(np.float32)
     return np.ascontiguousarray(square[..., peer_order(sizes)]), square, twiddle
@@ -128,18 +129,17 @@
         jnp.concatenate([recv_ref[pl.ds(2 * c + s, n, stride=4), :] for s in range(2)], axis=1)
         for c in range(2)
     ]
-    re, im = split_two(parts[0]), split_two(parts[1])
-    cos = (left_ref[0, 0], left_ref[0, 1])
-    sin = (left_ref[1, 0], left_ref[1, 1])
-    u_re = dot3(cos, re, NN) - dot3(sin, im, NN)
-    u_im = dot3(sin, re, NN) + dot3(cos, im, NN)
+    tables = [(left_ref[i, 0], left_ref[i, 1]) for i in range(3)]
+    factors = [split_two(x) for x in (parts[0] + parts[1], parts[0], parts[1])]
+    both, more, less = [dot3(t, x, NN) for t, x in zip(tables, factors)]
+    u_re, u_im = both - less, both + more
     t_re, t_im = twiddle_ref[0], twiddle_ref[1]
-    re = split_two(u_re * t_re - u_im * t_im)
-    im = split_two(u_re * t_im + u_im * t_re)
-    cos = (right_ref[0, 0], right_ref[0, 1])
-    sin = (right_ref[1, 0], right_ref[1, 1])
-    v_re = dot3(re, cos, NN) - dot3(im, sin, NN)
-    v_im = dot3(re, sin, NN) + dot3(im, cos, NN)
+    re = u_re * t_re - u_im * t_im
+    im = u_re * t_im + u_im * t_re
+    tables = [(right_ref[i, 0], right_ref[i, 1]) for i in range(3)]
+    factors = [split_two(x) for x in (re + im, re, im)]
+    both, more, less = [dot3(x, t, NN) for t, x in zip(tables, factors)]
+    v_re, v_im = both - less, both + more
     power = (v_re * v_re + v_im * v_im) * scale
     half = n // 2
     picks = []

time: 61.3 us -> 61 us (level)
  no operation moved by 1% of the time
where the time goes in v10:
time: 61 us; the launch traced here: 60.9 us
  blocking collectives  52.2 us (86%)
  Pallas kernels  4.79 us (8%)
  starting transfers between devices  1.6 us (3%)
  waiting for transfers between devices  0.82 us (1%)
  other arithmetic  0.71 us (1%)
  between operations  0.69 us (1%)
    all_to_all x1, blocking collectives, local(): got = lax.all_to_all(sent, PEERS, 0, 0, tiled=True)  35.8 us
    all_to_all x1, blocking collectives, local(): sums = lax.all_to_all(sums, CHIPS, 0, 0, tiled=True)  16.4 us
    pallas_call x1, Pallas kernels, plane_call(): pl.pallas_call(functools.partial(plane_kernel, scale, unit), out_shape=(j...  3.04 us
    pallas_call x1, Pallas kernels, depth_call(): pl.pallas_call(functools.partial(depth_kernel, step), in_specs=[pl.BlockS...  1.75 us
    ppermute x1, starting transfers between devices, local(): sums = sums + lax.ppermute(sums, CORE, [(0, 1), (1, 0)])  1.6 us
  transfers between devices with their start and end apart: 1, of which 1 were waited for; matrix products, arithmetic and copies ran while one was open for 0% of the time, Pallas kernels for 0%

profile of v10, /device:TPU:1, one launch (start us, length us, event | category | flops | bytes accessed | tf_op | source)
XLA Modules:
  0.0 60.9 jit_solution(3421562212789111611)
XLA Ops:
  0.6 0.0 copy-start.1
  0.6 0.0 copy-start.2
  0.7 1.7 %depth.1 = f32[1024,128]{1,0:T(8,128)S(1)} custom-call(f32[256,512]{1,0:T(8,128)} %bitcast.9, bf16[2,2,256,256]{3,2,1,0:T(8,128)(2,1)} %constant.10.clone.table_hbm), custom_call_target="tpu_custom_call" | custom-call | tf_op jit(solution)/shard_map/depth/pallas_call | solution.py:189
  2.4 0.0 copy-start
  2.4 0.0 copy-start.3
  2.4 35.8 %all_to_all.10 = f32[256,4,128]{2,1,0:T(4,128)S(1)} all-to-all(f32[256,4,128]{2,1,0:T(4,128)S(1)} %bitcast.6), channel_id=1, replica_groups=mesh['row_0'=4,'row_1'=2,'row_2'=2,'col_0'=2,'col_1'=4,'col_2'=2] {'row_..., dimensions={0} | all-to-all | bytes 1048576 | tf_op jit(solution)/shard_map/all_to_all | solution.py:230
  38.2 0.0 copy-done.1
  38.2 0.0 copy-done.2
  38.3 0.0 copy-done
  38.3 0.0 copy-done.3
  38.3 3.0 %plane.1 = (f32[256,256]{1,0:T(8,128)}, f32[2,128]{1,0:T(2,128)S(1)}) custom-call(f32[1024,128]{1,0:T(8,128)S(1)} %bitcast.7, bf16[3,2,256,256]{3,2,1,0:T(8,128)(2,1)S(1)} %copy-done.1, bf16[3,2,256,256]{3,2,1,0:T(8,128)(2,1)S(1)} %copy-done, f32[2,256,256]{2,1,0:T(8,128)S(1)} %copy-done.2, s32[256,256]{1,0:T(8,128)S(1)} %bitcast.8), custom_call_target="tpu_custom_call" | custom-call | tf_op jit(solution)/shard_map/plane/pallas_call | solution.py:205
  41.3 1.6 %collective-permute-start = (f32[2,128]{1,0:T(2,128)S(1)}, f32[2,128]{1,0:T(2,128)S(1)}, u32[]{:S(2)}, u32[]{:S(2)}) collective-permute-start(f32[2,128]{1,0:T(2,128)S(1)} %get-tuple-element.5), channel_id=1, source_target_pairs={{0,16},{16,0},{1,17},{17,1},{2,18},{18,2},{3,19},{19,3},{4,20},{20... | collective-permute-start | bytes 3080 | tf_op jit(solution)/shard_map/ppermute | solution.py:233
  42.9 0.8 %collective-permute-done = f32[2,128]{1,0:T(2,128)S(1)} collective-permute-done((f32[2,128]{1,0:T(2,128)S(1)}, f32[2,128]{1,0:T(2,128)S(1)}, u32[]{:S(2)}, u32[]{:S(2)}) %collective-permute-start) | collective-permute-done | bytes 1056 | tf_op jit(solution)/shard_map/ppermute | solution.py:233
  43.8 16.4 %all_to_all.11 = f32[128,2,128]{2,1,0:T(2,128)S(1)} all-to-all(f32[128,2,128]{2,1,0:T(2,128)S(1)} %broadcast_in_dim.3), channel_id=1, replica_groups=mesh['row_0'=4,'row_1'=2,'row_2'=2,'col_0'=2,'col_1'=4,'col_2'=2] {'col_..., dimensions={0} | all-to-all | bytes 262144 | tf_op jit(solution)/shard_map/all_to_all | solution.py:236
  60.1 0.7 %reduce_sum.9 = f32[2,128]{1,0:T(2,128)} reduce(f32[128,2,128]{2,1,0:T(2,128)S(1)} %all_to_all.11, f32[]{:T(128)} %constant.4.clone.1), dimensions={0}, to_apply=%region_0.0 | reduce | flops 32512 | bytes 132100 | tf_op jit(solution)/shard_map/reduce_sum | solution.py:237
  (2 shorter events, 0.0 us)
Async XLA Ops:
  0.6 37.6 %copy-start.1 = (bf16[3,2,256,256]{3,2,1,0:T(8,128)(2,1)S(1)}, bf16[3,2,256,256]{3,2,1,0:T(8,128)(2,1)}, u32[]{:S(2)}) copy-start(bf16[3,2,256,256]{3,2,1,0:T(8,128)(2,1)} %constant.11.clone.left_ref) | copy-start | bytes 2359300
  0.6 37.6 %copy-start.2 = (f32[2,256,256]{2,1,0:T(8,128)S(1)}, f32[2,256,256]{2,1,0:T(8,128)}, u32[]{:S(2)}) copy-start(f32[2,256,256]{2,1,0:T(8,128)} %constant.13.clone.twiddle_ref) | copy-start | bytes 1572868
  2.4 35.8 %copy-start = (bf16[3,2,256,256]{3,2,1,0:T(8,128)(2,1)S(1)}, bf16[3,2,256,256]{3,2,1,0:T(8,128)(2,1)}, u32[]{:S(2)}) copy-start(bf16[3,2,256,256]{3,2,1,0:T(8,128)(2,1)} %constant.12.clone.right_ref) | copy-start | bytes 2359300
  2.4 35.8 %copy-start.3 = (s32[1,256,256]{2,1,0:T(8,128)S(1)}, s32[1,256,256]{2,1,0:T(8,128)}, u32[]{:S(2)}) copy-start(s32[1,256,256]{2,1,0:T(8,128)} %param.7) | copy-start | bytes 786436
  41.3 2.4 %collective-permute-start = (f32[2,128]{1,0:T(2,128)S(1)}, f32[2,128]{1,0:T(2,128)S(1)}, u32[]{:S(2)}, u32[]{:S(2)}) collective-permute-start(f32[2,128]{1,0:T(2,128)S(1)} %get-tuple-element.5), channel_id=1, source_target_pairs={{0,16},{16,0},{1,17},{17,1},{2,18},{18,2},{3,19},{19,3},{4,20},{20... | collective-permute-start | bytes 3080 | tf_op jit(solution)/shard_map/ppermute | solution.py:233

commit v11 on v10

--- a/solution.py
+++ b/solution.py
@@ -16,7 +16,7 @@
 COL = ("col_0", "col_1", "col_2")
 ROW_COL = ROW + COL
 CORE = "row_2"
-PEERS = ("row_0", "col_0", "col_1", "row_1", "row_2", "col_2")
+PEERS = ("row_0", "col_0", "col_1", "row_1", "col_2", "row_2")
 CHIPS = ("col_1", "col_2", "col_0", "row_0", "row_1")
 F32 = jnp.float32
 BF16 = jnp.bfloat16

time: 61 us -> 61 us (level)
  no operation moved by 1% of the time
where the time goes in v11:
time: 61 us; the launch traced here: 60.8 us
  blocking collectives  52.6 us (86%)
  Pallas kernels  4.85 us (8%)
  starting transfers between devices  1.09 us (2%)
  waiting for transfers between devices  0.82 us (1%)
  other arithmetic  0.71 us (1%)
  between operations  0.69 us (1%)
    all_to_all x1, blocking collectives, local(): got = lax.all_to_all(sent, PEERS, 0, 0, tiled=True)  36.3 us
    all_to_all x1, blocking collectives, local(): sums = lax.all_to_all(sums, CHIPS, 0, 0, tiled=True)  16.2 us
    pallas_call x1, Pallas kernels, plane_call(): pl.pallas_call(functools.partial(plane_kernel, scale, unit), out_shape=(j...  3.04 us
    pallas_call x1, Pallas kernels, depth_call(): pl.pallas_call(functools.partial(depth_kernel, step), in_specs=[pl.BlockS...  1.81 us
  transfers between devices with their start and end apart: 1, of which 1 were waited for; matrix products, arithmetic and copies ran while one was open for 0% of the time, Pallas kernels for 0%

profile of v11, /device:TPU:1, one launch (start us, length us, event | category | flops | bytes accessed | tf_op | source)
XLA Modules:
  0.0 60.8 jit_solution(4664930441875715837)
XLA Ops:
  0.6 0.0 copy-start.1
  0.6 0.0 copy-start.2
  0.7 1.8 %depth.1 = f32[1024,128]{1,0:T(8,128)S(1)} custom-call(f32[256,512]{1,0:T(8,128)} %bitcast.9, bf16[2,2,256,256]{3,2,1,0:T(8,128)(2,1)} %constant.10.clone.table_hbm), custom_call_target="tpu_custom_call" | custom-call | tf_op jit(solution)/shard_map/depth/pallas_call | solution.py:189
  2.5 0.0 copy-start
  2.5 0.0 copy-start.3
  2.5 36.3 %all_to_all.10 = f32[256,4,128]{2,1,0:T(4,128)S(1)} all-to-all(f32[256,4,128]{2,1,0:T(4,128)S(1)} %bitcast.6), channel_id=1, replica_groups=mesh['row_0'=4,'row_1'=2,'row_2'=2,'col_0'=2,'col_1'=4,'col_2'=2] {'row_..., dimensions={0} | all-to-all | bytes 1048576 | tf_op jit(solution)/shard_map/all_to_all | solution.py:230
  38.8 0.0 copy-done.1
  38.8 0.0 copy-done.2
  38.8 0.0 copy-done
  38.8 0.0 copy-done.3
  38.8 3.0 %plane.1 = (f32[256,256]{1,0:T(8,128)}, f32[2,128]{1,0:T(2,128)S(1)}) custom-call(f32[1024,128]{1,0:T(8,128)S(1)} %bitcast.7, bf16[3,2,256,256]{3,2,1,0:T(8,128)(2,1)S(1)} %copy-done.1, bf16[3,2,256,256]{3,2,1,0:T(8,128)(2,1)S(1)} %copy-done, f32[2,256,256]{2,1,0:T(8,128)S(1)} %copy-done.2, s32[256,256]{1,0:T(8,128)S(1)} %bitcast.8), custom_call_target="tpu_custom_call" | custom-call | tf_op jit(solution)/shard_map/plane/pallas_call | solution.py:205
  41.9 1.1 %collective-permute-start = (f32[2,128]{1,0:T(2,128)S(1)}, f32[2,128]{1,0:T(2,128)S(1)}, u32[]{:S(2)}, u32[]{:S(2)}) collective-permute-start(f32[2,128]{1,0:T(2,128)S(1)} %get-tuple-element.5), channel_id=1, source_target_pairs={{0,16},{16,0},{1,17},{17,1},{2,18},{18,2},{3,19},{19,3},{4,20},{20... | collective-permute-start | bytes 3080 | tf_op jit(solution)/shard_map/ppermute | solution.py:233
  43.0 0.8 %collective-permute-done = f32[2,128]{1,0:T(2,128)S(1)} collective-permute-done((f32[2,128]{1,0:T(2,128)S(1)}, f32[2,128]{1,0:T(2,128)S(1)}, u32[]{:S(2)}, u32[]{:S(2)}) %collective-permute-start) | collective-permute-done | bytes 1056 | tf_op jit(solution)/shard_map/ppermute | solution.py:233
  43.8 16.2 %all_to_all.11 = f32[128,2,128]{2,1,0:T(2,128)S(1)} all-to-all(f32[128,2,128]{2,1,0:T(2,128)S(1)} %broadcast_in_dim.3), channel_id=1, replica_groups=mesh['row_0'=4,'row_1'=2,'row_2'=2,'col_0'=2,'col_1'=4,'col_2'=2] {'col_..., dimensions={0} | all-to-all | bytes 262144 | tf_op jit(solution)/shard_map/all_to_all | solution.py:236
  60.1 0.7 %reduce_sum.9 = f32[2,128]{1,0:T(2,128)} reduce(f32[128,2,128]{2,1,0:T(2,128)S(1)} %all_to_all.11, f32[]{:T(128)} %constant.4.clone.1), dimensions={0}, to_apply=%region_0.0 | reduce | flops 32512 | bytes 132100 | tf_op jit(solution)/shard_map/reduce_sum | solution.py:237
  (2 shorter events, 0.0 us)
Async XLA Ops:
  0.6 38.2 %copy-start.1 = (bf16[3,2,256,256]{3,2,1,0:T(8,128)(2,1)S(1)}, bf16[3,2,256,256]{3,2,1,0:T(8,128)(2,1)}, u32[]{:S(2)}) copy-start(bf16[3,2,256,256]{3,2,1,0:T(8,128)(2,1)} %constant.11.clone.left_ref) | copy-start | bytes 2359300
  0.6 38.2 %copy-start.2 = (f32[2,256,256]{2,1,0:T(8,128)S(1)}, f32[2,256,256]{2,1,0:T(8,128)}, u32[]{:S(2)}) copy-start(f32[2,256,256]{2,1,0:T(8,128)} %constant.13.clone.twiddle_ref) | copy-start | bytes 1572868
  2.5 36.4 %copy-start = (bf16[3,2,256,256]{3,2,1,0:T(8,128)(2,1)S(1)}, bf16[3,2,256,256]{3,2,1,0:T(8,128)(2,1)}, u32[]{:S(2)}) copy-start(bf16[3,2,256,256]{3,2,1,0:T(8,128)(2,1)} %constant.12.clone.right_ref) | copy-start | bytes 2359300
  2.5 36.3 %copy-start.3 = (s32[1,256,256]{2,1,0:T(8,128)S(1)}, s32[1,256,256]{2,1,0:T(8,128)}, u32[]{:S(2)}) copy-start(s32[1,256,256]{2,1,0:T(8,128)} %param.7) | copy-start | bytes 786436
  41.9 1.9 %collective-permute-start = (f32[2,128]{1,0:T(2,128)S(1)}, f32[2,128]{1,0:T(2,128)S(1)}, u32[]{:S(2)}, u32[]{:S(2)}) collective-permute-start(f32[2,128]{1,0:T(2,128)S(1)} %get-tuple-element.5), channel_id=1, source_target_pairs={{0,16},{16,0},{1,17},{17,1},{2,18},{18,2},{3,19},{19,3},{4,20},{20... | collective-permute-start | bytes 3080 | tf_op jit(solution)/shard_map/ppermute | solution.py:233

commit v12 on v11

--- a/solution.py
+++ b/solution.py
@@ -16,7 +16,7 @@
 COL = ("col_0", "col_1", "col_2")
 ROW_COL = ROW + COL
 CORE = "row_2"
-PEERS = ("row_0", "col_0", "col_1", "row_1", "col_2", "row_2")
+PEERS = ("row_0", "col_0", "col_1", "col_2", "row_1", "row_2")
 CHIPS = ("col_1", "col_2", "col_0", "row_0", "row_1")
 F32 = jnp.float32
 BF16 = jnp.bfloat16

time: 61 us -> 61 us (level)
  starting transfers between devices: 1.09 us -> 0.09 us
    ppermute x1, starting transfers between devices: 1.09 us -> 0.09 us  [local(): sums = sums + lax.ppermute(sums, CORE, [(0, 1), (1, 0)])]
where the time goes in v12:
time: 61 us; the launch traced here: 60.8 us
  blocking collectives  53.1 us (87%)
  Pallas kernels  5.01 us (8%)
  waiting for transfers between devices  1.15 us (2%)
  other arithmetic  0.71 us (1%)
  between operations  0.7 us (1%)
    all_to_all x1, blocking collectives, local(): got = lax.all_to_all(sent, PEERS, 0, 0, tiled=True)  36.6 us
    all_to_all x1, blocking collectives, local(): sums = lax.all_to_all(sums, CHIPS, 0, 0, tiled=True)  16.5 us
    pallas_call x1, Pallas kernels, plane_call(): pl.pallas_call(functools.partial(plane_kernel, scale, unit), out_shape=(j...  3.04 us
    pallas_call x1, Pallas kernels, depth_call(): pl.pallas_call(functools.partial(depth_kernel, step), in_specs=[pl.BlockS...  1.97 us
  transfers between devices with their start and end apart: 1, of which 1 were waited for; matrix products, arithmetic and copies ran while one was open for 0% of the time, Pallas kernels for 0%

profile of v12, /device:TPU:1, one launch (start us, length us, event | category | flops | bytes accessed | tf_op | source)
XLA Modules:
  0.0 60.8 jit_solution(6905316431455570476)
XLA Ops:
  0.6 0.0 copy-start.1
  0.6 0.0 copy-start.2
  0.7 2.0 %depth.1 = f32[1024,128]{1,0:T(8,128)S(1)} custom-call(f32[256,512]{1,0:T(8,128)} %bitcast.9, bf16[2,2,256,256]{3,2,1,0:T(8,128)(2,1)} %constant.10.clone.table_hbm), custom_call_target="tpu_custom_call" | custom-call | tf_op jit(solution)/shard_map/depth/pallas_call | solution.py:189
  2.6 0.0 copy-start
  2.6 0.0 copy-start.3
  2.7 36.6 %all_to_all.10 = f32[256,4,128]{2,1,0:T(4,128)S(1)} all-to-all(f32[256,4,128]{2,1,0:T(4,128)S(1)} %bitcast.6), channel_id=1, replica_groups=mesh['row_0'=4,'row_1'=2,'row_2'=2,'col_0'=2,'col_1'=4,'col_2'=2] {'row_..., dimensions={0} | all-to-all | bytes 1048576 | tf_op jit(solution)/shard_map/all_to_all | solution.py:230
  39.3 0.0 copy-done.1
  39.3 0.0 copy-done.2
  39.3 0.0 copy-done
  39.3 0.0 copy-done.3
  39.3 3.0 %plane.1 = (f32[256,256]{1,0:T(8,128)}, f32[2,128]{1,0:T(2,128)S(1)}) custom-call(f32[1024,128]{1,0:T(8,128)S(1)} %bitcast.7, bf16[3,2,256,256]{3,2,1,0:T(8,128)(2,1)S(1)} %copy-done.1, bf16[3,2,256,256]{3,2,1,0:T(8,128)(2,1)S(1)} %copy-done, f32[2,256,256]{2,1,0:T(8,128)S(1)} %copy-done.2, s32[256,256]{1,0:T(8,128)S(1)} %bitcast.8), custom_call_target="tpu_custom_call" | custom-call | tf_op jit(solution)/shard_map/plane/pallas_call | solution.py:205
  42.3 0.1 collective-permute-start
  42.4 1.1 %collective-permute-done = f32[2,128]{1,0:T(2,128)S(1)} collective-permute-done((f32[2,128]{1,0:T(2,128)S(1)}, f32[2,128]{1,0:T(2,128)S(1)}, u32[]{:S(2)}, u32[]{:S(2)}) %collective-permute-start) | collective-permute-done | bytes 1056 | tf_op jit(solution)/shard_map/ppermute | solution.py:233
  43.6 16.5 %all_to_all.11 = f32[128,2,128]{2,1,0:T(2,128)S(1)} all-to-all(f32[128,2,128]{2,1,0:T(2,128)S(1)} %broadcast_in_dim.3), channel_id=1, replica_groups=mesh['row_0'=4,'row_1'=2,'row_2'=2,'col_0'=2,'col_1'=4,'col_2'=2] {'col_..., dimensions={0} | all-to-all | bytes 262144 | tf_op jit(solution)/shard_map/all_to_all | solution.py:236
  60.1 0.7 %reduce_sum.9 = f32[2,128]{1,0:T(2,128)} reduce(f32[128,2,128]{2,1,0:T(2,128)S(1)} %all_to_all.11, f32[]{:T(128)} %constant.4.clone.1), dimensions={0}, to_apply=%region_0.0 | reduce | flops 32512 | bytes 132100 | tf_op jit(solution)/shard_map/reduce_sum | solution.py:237
  (2 shorter events, 0.0 us)
Async XLA Ops:
  0.6 38.6 %copy-start.1 = (bf16[3,2,256,256]{3,2,1,0:T(8,128)(2,1)S(1)}, bf16[3,2,256,256]{3,2,1,0:T(8,128)(2,1)}, u32[]{:S(2)}) copy-start(bf16[3,2,256,256]{3,2,1,0:T(8,128)(2,1)} %constant.11.clone.left_ref) | copy-start | bytes 2359300
  0.6 38.6 %copy-start.2 = (f32[2,256,256]{2,1,0:T(8,128)S(1)}, f32[2,256,256]{2,1,0:T(8,128)}, u32[]{:S(2)}) copy-start(f32[2,256,256]{2,1,0:T(8,128)} %constant.13.clone.twiddle_ref) | copy-start | bytes 1572868
  2.6 36.6 %copy-start = (bf16[3,2,256,256]{3,2,1,0:T(8,128)(2,1)S(1)}, bf16[3,2,256,256]{3,2,1,0:T(8,128)(2,1)}, u32[]{:S(2)}) copy-start(bf16[3,2,256,256]{3,2,1,0:T(8,128)(2,1)} %constant.12.clone.right_ref) | copy-start | bytes 2359300
  2.6 36.6 %copy-start.3 = (s32[1,256,256]{2,1,0:T(8,128)S(1)}, s32[1,256,256]{2,1,0:T(8,128)}, u32[]{:S(2)}) copy-start(s32[1,256,256]{2,1,0:T(8,128)} %param.7) | copy-start | bytes 786436
  42.3 1.2 %collective-permute-start = (f32[2,128]{1,0:T(2,128)S(1)}, f32[2,128]{1,0:T(2,128)S(1)}, u32[]{:S(2)}, u32[]{:S(2)}) collective-permute-start(f32[2,128]{1,0:T(2,128)S(1)} %get-tuple-element.5), channel_id=1, source_target_pairs={{0,16},{16,0},{1,17},{17,1},{2,18},{18,2},{3,19},{19,3},{4,20},{20... | collective-permute-start | bytes 3080 | tf_op jit(solution)/shard_map/ppermute | solution.py:233
